TPU v7x, 32 devices: a 4x4x1 block of a 4x4x8 slice. The times are simulated.
32 devices in a mesh: dp: 1 (over z), tp: 4 (over y), sp: 8 (over x, core).
Axes of the slice: x: 4, y: 4, z: 1, core: 2. Of those that a mesh axis runs over, the one named last changes fastest.
The devices are a block of a 4x4x8 slice.
Arguments:
- tokens: bfloat16 [16384, 768], P(('dp', 'sp'))
- glob_pos: int32 [1024], P('dp')
- w_query: bfloat16 [768, 12, 64], P(None, 'tp')
- w_key: bfloat16 [768, 12, 64], P(None, 'tp')
- w_value: bfloat16 [768, 12, 64], P(None, 'tp')
- w_out: bfloat16 [12, 64, 768], P('tp')
- w_up: bfloat16 [768, 3072], P(None, 'tp')
- w_down: bfloat16 [3072, 768], P('tp')
Outputs:
- output: bfloat16 [16384, 768], P(('dp', 'sp'))
All inputs are finite; a program needn't handle non-finite values.
Results may differ from a plain program's by a relative error of at most 0.00772977.
Values are sent between devices in bfloat16 or wider.
A program may use at most 768 MiB of HBM per device.

v0:
```python
import jax
import jax.numpy as jnp
from jax import lax
from jax.sharding import PartitionSpec as P
import math

WIN = 256


def local_window(q_rows, k_ext, v_ext, k_glob, v_glob, glob_pos, first_row, seq_len):
    n_rows, n_heads, head_dim = q_rows.shape
    scale = 1.0 / math.sqrt(head_dim)
    q_block = 128
    key_span = q_block + 2 * WIN

    def one_block(blk_index):
        start = blk_index * q_block
        q_blk = lax.dynamic_slice_in_dim(q_rows, start, q_block)
        k_blk = lax.dynamic_slice_in_dim(k_ext, start, key_span)
        v_blk = lax.dynamic_slice_in_dim(v_ext, start, key_span)
        q_pos = first_row + start + jnp.arange(q_block)
        k_pos = first_row + start - WIN + jnp.arange(key_span)
        k_is_glob = jnp.any(k_pos[:, None] == glob_pos[None, :], axis=1)
        k_ok = (k_pos >= 0) & (k_pos < seq_len) & jnp.logical_not(k_is_glob)
        allowed = (jnp.abs(q_pos[:, None] - k_pos[None, :]) <= WIN) & k_ok[None, :]
        s_win = jnp.einsum('qhe,khe->hqk', q_blk, k_blk, preferred_element_type=jnp.float32) * scale
        s_win = jnp.where(allowed[None], s_win, -jnp.inf)
        s_glob = jnp.einsum('qhe,ghe->hqg', q_blk, k_glob, preferred_element_type=jnp.float32) * scale
        row_max = jnp.maximum(jnp.max(s_win, axis=2, keepdims=True), jnp.max(s_glob, axis=2, keepdims=True))
        e_win = jnp.exp(s_win - row_max)
        e_glob = jnp.exp(s_glob - row_max)
        total = jnp.sum(e_win, axis=2, keepdims=True) + jnp.sum(e_glob, axis=2, keepdims=True)
        p_win = (e_win / total).astype(jnp.bfloat16)
        p_glob = (e_glob / total).astype(jnp.bfloat16)
        blk_out = jnp.einsum('hqk,khe->qhe', p_win, v_blk, preferred_element_type=jnp.float32)
        blk_out = blk_out + jnp.einsum('hqg,ghe->qhe', p_glob, v_glob, preferred_element_type=jnp.float32)
        return blk_out.astype(jnp.bfloat16)

    blocks = lax.map(one_block, jnp.arange(n_rows // q_block))
    return blocks.reshape(n_rows, n_heads, head_dim)


def pick_rows(row_array, safe_idx, owned):
    picked = jnp.take(row_array, safe_idx, axis=0)
    return jnp.where(owned[:, None, None], picked, 0)


def global_queries(q_glob, k_rows, v_rows):
    scale = 1.0 / math.sqrt(q_glob.shape[2])
    scores = jnp.einsum('ghe,rhe->hgr', q_glob, k_rows, preferred_element_type=jnp.float32) * scale
    glob_max = lax.pmax(jnp.max(scores, axis=2, keepdims=True), 'sp')
    exp_scores = jnp.exp(scores - glob_max)
    glob_sum = lax.psum(jnp.sum(exp_scores, axis=2, keepdims=True), 'sp')
    prob_rows = (exp_scores / glob_sum).astype(jnp.bfloat16)
    part_out = jnp.einsum('hgr,rhe->ghe', prob_rows, v_rows, preferred_element_type=jnp.float32)
    return lax.psum(part_out, 'sp').astype(jnp.bfloat16)


def solution(mesh):
    n_seq = mesh.shape['sp']
    to_right = [(i, i + 1) for i in range(n_seq - 1)]
    to_left = [(i + 1, i) for i in range(n_seq - 1)]

    def device_layer(tokens, glob_pos, w_query, w_key, w_value, w_out, w_up, w_down):
        n_rows = tokens.shape[0]
        first_row = lax.axis_index('sp') * n_rows
        q_rows = jnp.einsum('rd,dhe->rhe', tokens, w_query, preferred_element_type=jnp.float32).astype(jnp.bfloat16)
        k_rows = jnp.einsum('rd,dhe->rhe', tokens, w_key, preferred_element_type=jnp.float32).astype(jnp.bfloat16)
        v_rows = jnp.einsum('rd,dhe->rhe', tokens, w_value, preferred_element_type=jnp.float32).astype(jnp.bfloat16)
        left_k, left_v = lax.ppermute((k_rows[n_rows - WIN:], v_rows[n_rows - WIN:]), 'sp', to_right)
        right_k, right_v = lax.ppermute((k_rows[:WIN], v_rows[:WIN]), 'sp', to_left)
        k_ext = jnp.concatenate([left_k, k_rows, right_k], axis=0)
        v_ext = jnp.concatenate([left_v, v_rows, right_v], axis=0)
        local_idx = glob_pos - first_row
        owned = (local_idx >= 0) & (local_idx < n_rows)
        safe_idx = jnp.clip(local_idx, 0, n_rows - 1)
        picked = (pick_rows(q_rows, safe_idx, owned), pick_rows(k_rows, safe_idx, owned), pick_rows(v_rows, safe_idx, owned))
        q_glob, k_glob, v_glob = lax.psum(picked, 'sp')
        attn_rows = local_window(q_rows, k_ext, v_ext, k_glob, v_glob, glob_pos, first_row, n_rows * n_seq)
        glob_out = global_queries(q_glob, k_rows, v_rows)
        attn_rows = attn_rows.at[jnp.where(owned, local_idx, n_rows)].set(glob_out, mode='drop')
        mixed = lax.psum(jnp.einsum('rhe,hed->rd', attn_rows, w_out, preferred_element_type=jnp.float32), 'tp')
        hidden = (tokens.astype(jnp.float32) + mixed).astype(jnp.bfloat16)
        gelu_rows = jax.nn.gelu(jnp.dot(hidden, w_up, preferred_element_type=jnp.float32), approximate=True).astype(jnp.bfloat16)
        down_sum = lax.psum(jnp.dot(gelu_rows, w_down, preferred_element_type=jnp.float32), 'tp')
        return (hidden.astype(jnp.float32) + down_sum).astype(jnp.bfloat16)

    row_spec = P(('dp', 'sp'), None)
    head_spec = P(None, 'tp', None)
    in_specs = (row_spec, P('dp'), head_spec, head_spec, head_spec, P('tp', None, None), P(None, 'tp'), P('tp', None))
    return jax.shard_map(device_layer, mesh=mesh, in_specs=in_specs, out_specs=row_spec, check_vma=False)
```

profile of v0, /device:TPU:97, one launch (start us, length us, event | category | flops | bytes accessed | tf_op | source)
XLA Modules:
  0.0 684.8 jit_solution(9457699608690274961)
XLA Ops:
  6.6 3.2 fusion.46
  10.6 4.6 collective-permute-start.2
  19.2 3.7 collective-permute-start
  24.8 2.5 copy.19
  30.4 9.1 %gather_fusion = bf16[1024,3,64]{2,1,0:T(4,128)(2,1)} fusion(bf16[2048,3,64]{2,1,0:T(4,128)(2,1)} %copy.19, s32[1024]{0:T(1024)S(1)} %get-tuple-element.164), kind=kCustom, calls=%fused_computation.clone | custom fusion | bytes 790528 | tf_op jit(solution)/shard_map/jit(_take)/gather | solution.py:44
  41.7 9.1 %gather_fusion.1 = bf16[1024,3,64]{2,1,0:T(4,128)(2,1)} fusion(bf16[2048,3,64]{2,1,0:T(4,128)(2,1)} %copy.21, s32[1024]{0:T(1024)S(1)} %get-tuple-element.164), kind=kCustom, calls=%fused_computation.1.clone | custom fusion | bytes 790528 | tf_op jit(solution)/shard_map/jit(_take)/gather | solution.py:44
  53.0 3.0 fusion.45
  56.1 2.5 copy.24
  58.6 9.1 %gather_fusion.2 = bf16[1024,3,64]{2,1,0:T(4,128)(2,1)} fusion(bf16[2048,3,64]{2,1,0:T(4,128)(2,1)} %copy.24, s32[1024]{0:T(1024)S(1)} %get-tuple-element.164), kind=kCustom, calls=%fused_computation.2.clone | custom fusion | bytes 790528 | tf_op jit(solution)/shard_map/jit(_take)/gather | solution.py:44
  76.3 54.9 %all-reduce.10.cloned.1.call-done = (bf16[1024,3,64]{0,2,1:T(8,128)(2,1)}, bf16[1024,3,64]{0,2,1:T(8,128)(2,1)}, bf16[1024,3,64]{0,2,1:T(8,128)(2,1)}) async-done(((bf16[1024,3,64]{0,2,1:T(8,128)(2,1)}, bf16[1024,3,64]{0,2,1:T(8,128)(2,1)}, bf16[1024,3,64]{0,2,1:T(8,128)(2,1)}), (bf16[1024,3,64]{0,2,1:T(8,128)(2,1)}, bf16[1024,3,64]{0,2,1:T(8,128)(2,1)}, ...) | async-done | bytes 1179664 | tf_op jit(solution)/shard_map/psum | solution.py:78
  131.3 11.7 %multiply_reduce_fusion = (f32[3,1024]{1,0:T(4,128)}, f32[3,1024,2048]{2,1,0:T(8,128)}) fusion(bf16[1024,3,64]{0,2,1:T(8,128)(2,1)} %get-tuple-element.154, bf16[2048,3,64]{0,2,1:T(8,128)(2,1)S(1)} %convert_element_type.55), kind=kOutput, calls=%fused_computation.34 | convolution fusion | flops 817886208 | bytes 26357760 | tf_op jit(solution)/shard_map/ghe,rhe->hgr/dot_general | solution.py:50
  142.9 23.6 %pmax.7 = f32[3,1024]{1,0:T(4,128)S(1)} all-reduce(f32[3,1024]{1,0:T(4,128)} %get-tuple-element.170), channel_id=1, replica_groups=mesh['dp'=1,'tp'=4,'sp'=8] {'sp'}, use_global_device_ids=true, to_apply=%region_11.13 | all-reduce | flops 3072 | bytes 24576 | tf_op jit(solution)/shard_map/pmax | solution.py:51
  166.6 10.8 %fusion.15 = f32[3,1024]{1,0:T(4,128)S(1)} fusion(f32[3,1024,2048]{2,1,0:T(8,128)} %get-tuple-element.171, f32[3,1024]{1,0:T(4,128)S(1)} %pmax.7), kind=kLoop, calls=%fused_computation.35 | loop fusion | flops 18871296 | bytes 25190400 | tf_op jit(solution)/shard_map/reduce_sum | solution.py:53
  177.3 23.6 %psum.52 = f32[3,1024]{1,0:T(4,128)S(1)} all-reduce(f32[3,1024]{1,0:T(4,128)S(1)} %fusion.15), channel_id=1, replica_groups=mesh['dp'=1,'tp'=4,'sp'=8] {'sp'}, use_global_device_ids=true, to_apply=%region_13.15 | all-reduce | flops 3072 | bytes 24576 | tf_op jit(solution)/shard_map/psum | solution.py:53
  201.0 11.7 %fusion.32 = f32[1024,3,64]{0,2,1:T(8,128)} fusion(bf16[2048,3,64]{0,2,1:T(8,128)(2,1)S(1)} %convert_element_type.53, f32[3,1024,2048]{2,1,0:T(8,128)} %get-tuple-element.171, f32[3,1024]{1,0:T(4,128)S(1)} %psum.52, f32[3,1024]{1,0:T(4,128)S(1)} %pmax.7), kind=kOutput, calls=%fused_computation.55 | convolution fusion | flops 830472192 | bytes 26763264 | tf_op jit(solution)/shard_map/hgr,rhe->ghe/dot_general | solution.py:55
  212.7 30.4 %all-reduce.11 = bf16[1024,3,64]{0,2,1:T(8,128)(2,1)S(1)} all-reduce(f32[1024,3,64]{0,2,1:T(8,128)} %fusion.32), channel_id=1, replica_groups=mesh['dp'=1,'tp'=4,'sp'=8] {'sp'}, use_global_device_ids=true, to_apply=%region_14.16 | all-reduce | flops 196608 | bytes 1179648 | tf_op jit(solution)/shard_map/psum | solution.py:56
  244.5 114.4 %while.12 = (s32[]{:T(128)}, bf16[16,128,3,64]{1,3,2,0:T(8,128)(2,1)}, s32[16]{0:T(128)S(1)}, bf16[2560,3,64]{0,2,1:T(8,128)(2,1)}, s32[]{:T(128)}, /*index=5*/s...) while((s32[]{:T(128)}, ...), condition=%wide.region_8.10_spmd, body=%wide.region_2.9_spmd.sunk | while | flops 169987200 | bytes 11067192 | solution.py:39
  358.9 2.8 copy.23
  361.8 48.9 %scatter_fusion = bf16[2048,3,64]{2,1,0:T(4,128)(2,1)S(1)} fusion(bf16[2048,3,64]{2,1,0:T(4,128)(2,1)S(1)} %bitcast.54, s32[1024]{0:T(1024)S(1)} %get-tuple-element.163, bf16[1024,3,64]{2,1,0:T(4,128)(2,1)} %copy.26), kind=kCustom, calls=%fused_computation.3 | custom fusion | bytes 1183744 | tf_op jit(solution)/shard_map/scatter | solution.py:81
  410.7 4.7 convolution_bitcast_fusion.2
  415.4 123.1 %all-reduce.6.cloned.1.call-done = f32[2048,768]{1,0:T(8,128)} async-done(((f32[2048,768]{1,0:T(8,128)}), f32[2048,768]{1,0:T(8,128)}) %all-reduce.6.cloned.1.call-update) | async-done | bytes 6291472 | tf_op jit(solution)/shard_map/psum | solution.py:82
  538.5 9.8 %fusion.25 = f32[2048,768]{1,0:T(8,128)} fusion(bf16[768,768]{1,0:T(8,128)(2,1)S(1)} %copy-done, bf16[768,768]{1,0:T(8,128)(2,1)S(1)} %copy-done.6, f32[2048,768]{1,0:T(8,128)} %all-reduce.6.cloned.1.call-done, bf16[2048,768]{1,0:T(8,128)(2,1)} %param.12), kind=kOutput, calls=%fused_computation.49 | convolution fusion | flops 4850712576 | bytes 18087936 | tf_op jit(solution)/shard_map/dot_general | solution.py:85
  548.4 121.6 %all-reduce.8.cloned.1.call-done = f32[2048,768]{1,0:T(8,128)} async-done(((f32[2048,768]{1,0:T(8,128)}), f32[2048,768]{1,0:T(8,128)}) %all-reduce.8.cloned.1.call-update) | async-done | bytes 6291472 | tf_op jit(solution)/shard_map/psum | solution.py:85
  670.0 8.2 %add_convert_fusion = bf16[2048,768]{1,0:T(8,128)(2,1)} fusion(f32[2048,768]{1,0:T(8,128)} %all-reduce.8.cloned.1.call-done, f32[2048,768]{1,0:T(8,128)} %all-reduce.6.cloned.1.call-done, bf16[2048,768]{1,0:T(8,128)(2,1)} %param.12), kind=kLoop, calls=%fused_computation.46 | loop fusion | flops 9437184 | bytes 18874368 | tf_op jit(solution)/shard_map/convert_element_type | solution.py:86
  (300 shorter events, 127.0 us)
Async XLA Ops:
  6.5 532.0 %copy-start = (bf16[768,768]{1,0:T(8,128)(2,1)S(1)}, bf16[768,768]{1,0:T(8,128)(2,1)}, u32[]{:S(2)}) copy-start(bf16[768,768]{1,0:T(8,128)(2,1)} %param.19) | copy-start | bytes 3538948
  6.6 124.7 %all-reduce.10.cloned.1.call-start = ((), (), s32[]{:S(2)}) async-start(), calls=%async_computation.2 | async-start | bytes 2359296 | tf_op jit(solution)/shard_map/psum | solution.py:78
  6.6 10.6 %copy-start.1 = (bf16[2048,768]{1,0:T(8,128)(2,1)S(1)}, bf16[2048,768]{1,0:T(8,128)(2,1)}, u32[]{:S(2)}) copy-start(bf16[2048,768]{1,0:T(8,128)(2,1)} %param.12) | copy-start | bytes 9437188
  6.6 10.6 %copy-start.3 = (bf16[768,3,64]{0,2,1:T(8,128)(2,1)S(1)}, bf16[768,3,64]{0,2,1:T(8,128)(2,1)}, u32[]{:S(2)}) copy-start(bf16[768,3,64]{0,2,1:T(8,128)(2,1)} %param.16) | copy-start | bytes 884740
  10.6 61.7 %collective-permute-start.2 = (bf16[256,3,64]{0,2,1:T(8,128)(2,1)}, bf16[256,3,64]{0,2,1:T(8,128)(2,1)}, u32[]{:S(2)}, u32[]{:S(2)}) collective-permute-start(bf16[256,3,64]{0,2,1:T(8,128)(2,1)} %get-tuple-element.159), channel_id=1, source_target_pairs={{0,1},{1,2},{2,3},{3,4},{4,5},{5,6},{6,7},{8,9},{9,10},{10,11},{11... | collective-permute-start | bytes 294920 | tf_op jit(solution)/shard_map/ppermute | solution.py:70
  15.2 57.1 %collective-permute-start.3 = (bf16[256,3,64]{0,2,1:T(8,128)(2,1)}, bf16[256,3,64]{0,2,1:T(8,128)(2,1)}, u32[]{:S(2)}, u32[]{:S(2)}) collective-permute-start(bf16[256,3,64]{0,2,1:T(8,128)(2,1)} %get-tuple-element.160), channel_id=1, source_target_pairs={{1,0},{2,1},{3,2},{4,3},{5,4},{6,5},{7,6},{9,8},{10,9},{11,10},{12... | collective-permute-start | bytes 294920 | tf_op jit(solution)/shard_map/ppermute | solution.py:71
  18.5 11.3 %copy-start.5 = (s32[1024]{0:T(1024)S(1)}, s32[1024]{0:T(1024)}, u32[]{:S(2)}) copy-start(s32[1024]{0:T(1024)} %param.13) | copy-start | bytes 12292
  19.2 55.2 %collective-permute-start = (bf16[256,3,64]{0,2,1:T(8,128)(2,1)}, bf16[256,3,64]{0,2,1:T(8,128)(2,1)}, u32[]{:S(2)}, u32[]{:S(2)}) collective-permute-start(bf16[256,3,64]{0,2,1:T(8,128)(2,1)} %get-tuple-element.161), channel_id=1, source_target_pairs={{0,1},{1,2},{2,3},{3,4},{4,5},{5,6},{6,7},{8,9},{9,10},{10,11},{11... | collective-permute-start | bytes 294920 | tf_op jit(solution)/shard_map/ppermute | solution.py:70
  22.8 51.6 %collective-permute-start.1 = (bf16[256,3,64]{0,2,1:T(8,128)(2,1)}, bf16[256,3,64]{0,2,1:T(8,128)(2,1)}, u32[]{:S(2)}, u32[]{:S(2)}) collective-permute-start(bf16[256,3,64]{0,2,1:T(8,128)(2,1)} %get-tuple-element.162), channel_id=1, source_target_pairs={{1,0},{2,1},{3,2},{4,3},{5,4},{6,5},{7,6},{9,8},{10,9},{11,10},{12... | collective-permute-start | bytes 294920 | tf_op jit(solution)/shard_map/ppermute | solution.py:71
  30.4 22.6 %copy-start.4 = (bf16[768,3,64]{0,2,1:T(8,128)(2,1)S(1)}, bf16[768,3,64]{0,2,1:T(8,128)(2,1)}, u32[]{:S(2)}) copy-start(bf16[768,3,64]{0,2,1:T(8,128)(2,1)} %param.14) | copy-start | bytes 884740
  72.2 466.3 %all-reduce.6.cloned.1.call-start = ((), (), s32[]{:S(2)}) async-start(), calls=%async_computation | async-start | bytes 12582912 | tf_op jit(solution)/shard_map/psum | solution.py:82
  201.0 43.5 %copy-start.2 = (bf16[1024,3,64]{0,2,1:T(8,128)(2,1)S(1)}, bf16[1024,3,64]{0,2,1:T(8,128)(2,1)}, u32[]{:S(2)}) copy-start(bf16[1024,3,64]{0,2,1:T(8,128)(2,1)} %get-tuple-element.249) | copy-start | bytes 1179652
  255.6 2.1 copy-start.7
  269.8 2.1 copy-start.7
  277.0 2.1 copy-start.7
  291.3 2.1 copy-start.7
  305.6 2.1 copy-start.7
  312.8 2.1 copy-start.7
  319.9 2.1 copy-start.7
  327.1 2.1 copy-start.7
  341.4 2.1 copy-start.7
  355.7 2.1 copy-start.7
  415.3 123.2 %copy-start.6 = (bf16[768,768]{1,0:T(8,128)(2,1)S(1)}, bf16[768,768]{1,0:T(8,128)(2,1)}, u32[]{:S(2)}) copy-start(bf16[768,768]{1,0:T(8,128)(2,1)} %param.18) | copy-start | bytes 3538948
  415.4 254.6 %all-reduce.8.cloned.1.call-start = ((), (), s32[]{:S(2)}) async-start(), calls=%async_computation.1 | async-start | bytes 12582912 | tf_op jit(solution)/shard_map/psum | solution.py:85
  (6 other events, 12.7 us)
Sparse Core Ops, SparseCore 0:
  72.4 58.8 all-reduce.9
  415.5 122.9 all-reduce.5
  548.5 121.4 all-reduce.7
where the time goes:
time: 691 us; the launch traced here: 685 us
  waiting for transfers between devices  300 us (43%)
  matrix products  116 us (17%)
  local copies, waits for them, and re-layouts  106 us (15%)
  blocking collectives  77.7 us (11%)
  other arithmetic  47.7 us (7%)
  between operations  13.3 us (2%)
  starting transfers between devices  12.3 us (2%)
  loops' own time  11.8 us (2%)
    psum x1, waiting for transfers between devices, device_layer(): lax.psum(jnp.einsum('rhe,hed->rd', attn_rows, w_out, preferred_element_ty...  123 us
    psum x1, waiting for transfers between devices, device_layer(): lax.psum(jnp.dot(gelu_rows, w_down, preferred_element_type=jnp.float32),...  122 us
    psum x1, waiting for transfers between devices, device_layer(): q_glob, k_glob, v_glob = lax.psum(picked, 'sp')  54.9 us
    scatter x1, local copies, waits for them, and re-layouts, device_layer(): attn_rows.at[jnp.where(owned, local_idx, n_rows)].set(glob_out, mode='drop')  48.9 us
    gather x6, local copies, waits for them, and re-layouts, pick_rows(): picked = jnp.take(row_array, safe_idx, axis=0)  33.8 us
    psum x1, blocking collectives, global_queries(): return lax.psum(part_out, 'sp').astype(jnp.bfloat16)  30.4 us
    psum x1, blocking collectives, global_queries(): glob_sum = lax.psum(jnp.sum(exp_scores, axis=2, keepdims=True), 'sp')  23.6 us
    pmax x1, blocking collectives, global_queries(): glob_max = lax.pmax(jnp.max(scores, axis=2, keepdims=True), 'sp')  23.6 us
  transfers between devices with their start and end apart: 7, of which 3 were waited for; matrix products, arithmetic and copies ran while one was open for 8% of the time, Pallas kernels for 0%

commit v1 on v0

v1 whole, which is shorter than its diff:
```python
import functools
import math

import jax
import jax.numpy as jnp
from jax import lax
from jax.experimental import pallas as pl
from jax.experimental.pallas import tpu as pltpu
from jax.sharding import PartitionSpec as P

WIN = 256
NEG = -1e38
BQ = 256
F32 = jnp.float32
BF16 = jnp.bfloat16
MESH = pl.DeviceIdType.MESH
NT = (((1,), (1,)), ((), ()))
TN = (((0,), (0,)), ((), ()))


def remote(src, dst, send, recv, where):
    return pltpu.make_async_remote_copy(src_ref=src, dst_ref=dst, send_sem=send, recv_sem=recv, device_id=where, device_id_type=MESH)


def attention_kernel(dims, x_ref, pick_ref, wqv_ref, wk_ref, kpad_ref, gpos_ref, wcat_ref,
                     o_ref, wr_ref,
                     halo, rs_recv, xg, qT, k_aug, vT, qgT, kg_aug, vgT, m_w, l_w, acc_w, part, part_recv, og_all, og_ext, o_loc,
                     halo_s, halo_r, rs_s, rs_r, ag_s, ag_r, agd_s, agd_r, pt_s, pt_r, og_s, og_r, a2a_s, a2a_r, loc_s,
                     wy_s, wy_r, wf_s, wf_r, wx_s, wx_r, wd_s, wd_r):
    n_sp, n_tp, n_heads, hd = dims
    n_rows = x_ref.shape[0]
    width = n_heads * hd
    n_x = n_sp // 2
    n_blk = n_rows // BQ
    s = lax.axis_index('sp')
    t = lax.axis_index('tp')
    core = s % 2
    chip = s // 2
    G = gpos_ref.shape[1]
    per = G // (n_sp * n_tp)
    wrows = wcat_ref.shape[0] // n_sp
    half = (wrows // 32) * 16

    def sp(d):
        return (s + d + n_sp) % n_sp

    def tp(d):
        return (t + d + n_tp) % n_tp

    bar = pltpu.get_barrier_semaphore()
    n_peers = 0
    for d in range(1, n_sp):
        pl.semaphore_signal(bar, inc=1, device_id={'sp': sp(d)}, device_id_type=MESH)
        n_peers += 1
    for dt in range(1, n_tp):
        for dx in range(n_x):
            pl.semaphore_signal(bar, inc=1, device_id={'sp': sp(2 * dx), 'tp': tp(dt)}, device_id_type=MESH)
            n_peers += 1
    pl.semaphore_wait(bar, n_peers)

    rs = [remote(pick_ref.at[sp(d)], rs_recv.at[s], rs_s.at[d - 1], rs_r.at[d - 1], {'sp': sp(d)}) for d in range(1, n_sp)]
    for c in rs:
        c.start()
    halo_c = [remote(x_ref.at[pl.ds(n_rows - WIN, WIN)], halo.at[0], halo_s.at[0], halo_r.at[0], {'sp': sp(1)}),
              remote(x_ref.at[pl.ds(0, WIN)], halo.at[1], halo_s.at[1], halo_r.at[1], {'sp': sp(-1)})]
    for c in halo_c:
        c.start()

    def wslice(piece):
        return pl.ds(pl.multiple_of(piece * wrows, 16), wrows)

    pieces = [s, sp(2)]
    wy = []
    for i, piece in enumerate(pieces):
        for j, (d, slot) in enumerate(((-1, 0), (1, 2))):
            wy.append(remote(wcat_ref.at[wslice(piece)], wr_ref.at[slot, wslice(piece)], wy_s.at[2 * i + j], wy_r.at[2 * i + j], {'tp': tp(d)}))

    def start_wy():
        for c in wy:
            c.start()

    wf = []
    for i, piece in enumerate(pieces):
        lo = pl.ds(pl.multiple_of(piece * wrows, 16), half)
        hi = pl.ds(pl.multiple_of(piece * wrows + half, 16), wrows - half)
        wf.append(remote(wr_ref.at[0, lo], wr_ref.at[1, lo], wf_s.at[2 * i], wf_r.at[2 * i], {'tp': tp(-1)}))
        wf.append(remote(wr_ref.at[2, hi], wr_ref.at[1, hi], wf_s.at[2 * i + 1], wf_r.at[2 * i + 1], {'tp': tp(1)}))
    wx = [remote(wr_ref.at[:, wslice(s)], wr_ref.at[:, wslice(s)], wx_s.at[0], wx_r.at[0], {'sp': sp(2)}),
          remote(wr_ref.at[:, wslice(sp(2))], wr_ref.at[:, wslice(sp(2))], wx_s.at[1], wx_r.at[1], {'sp': sp(-2)})]
    wx_in = [remote(wr_ref.at[:, wslice(sp(-2))], wr_ref.at[:, wslice(sp(-2))], wx_s.at[0], wx_r.at[0], {'sp': sp(2)}),
             remote(wr_ref.at[:, wslice(sp(4))], wr_ref.at[:, wslice(sp(4))], wx_s.at[1], wx_r.at[1], {'sp': sp(-2)})]
    partner = 2 * chip + 1 - core
    wd = [remote(wr_ref.at[:, wslice(sp(2 * j))], wr_ref.at[:, wslice(sp(2 * j))], wd_s.at[j], wd_r.at[j], {'sp': partner}) for j in range(4)]
    wd_in = [remote(wr_ref.at[:, wslice((partner + 2 * j) % n_sp)], wr_ref.at[:, wslice((partner + 2 * j) % n_sp)], wd_s.at[j], wd_r.at[j], {'sp': partner}) for j in range(4)]

    def project(rows, kdst, vdst, qdst, kdst_row, vcol, qcol):
        qv = lax.dot_general(wqv_ref[...], rows, NT, preferred_element_type=F32).astype(BF16)
        kk = jnp.dot(rows, wk_ref[...], preferred_element_type=F32).astype(BF16)
        kdst[kdst_row, pl.ds(0, width)] = kk
        vdst[:, vcol] = qv[width:]
        if qdst is not None:
            qdst[:, qcol] = (qv[:width].astype(F32) * (1.0 / math.sqrt(hd))).astype(BF16)

    def proj_block(b, carry):
        base = pl.multiple_of(b * BQ, BQ)
        ext = pl.multiple_of(b * BQ + WIN, BQ)
        project(x_ref[pl.ds(base, BQ)], k_aug, vT, qT, pl.ds(ext, BQ), pl.ds(ext, BQ), pl.ds(base, BQ))
        return carry

    k_aug[:, pl.ds(width, hd)] = kpad_ref[...]
    kg_aug[:, pl.ds(width, hd)] = jnp.zeros((G, hd), BF16)
    lax.fori_loop(0, n_blk, proj_block, 0)

    for c in rs:
        c.wait_recv()
    mine = core * (n_x * n_tp) + t * n_x + chip
    rs_recv[s] = pick_ref[s]
    xg[mine] = jnp.sum(rs_recv[...].astype(F32), axis=0).astype(BF16)
    ag = []
    for dt in range(n_tp):
        for dx in range(n_x):
            if dt or dx:
                j = dt * n_x + dx - 1
                ag.append(remote(xg.at[mine], xg.at[mine], ag_s.at[j], ag_r.at[j], {'sp': sp(2 * dx), 'tp': tp(dt)}))
    for c in ag:
        c.start()
    start_wy()
    for c in halo_c:
        c.wait_recv()
    project(halo[0], k_aug, vT, None, pl.ds(0, WIN), pl.ds(0, WIN), None)
    project(halo[1], k_aug, vT, None, pl.ds(n_rows + WIN, WIN), pl.ds(n_rows + WIN, WIN), None)

    flag_rows = (lax.broadcasted_iota(jnp.int32, (hd, BQ), 0) == 0).astype(F32).astype(BF16)

    def q_cols(src, h, cols, biased):
        parts = [src[pl.ds(h * hd, hd), cols]]
        if h:
            parts.insert(0, jnp.zeros((h * hd, BQ), BF16))
        if h + 1 < n_heads:
            parts.append(jnp.zeros(((n_heads - 1 - h) * hd, BQ), BF16))
        parts.append(flag_rows if biased else jnp.zeros((hd, BQ), BF16))
        return jnp.concatenate(parts, axis=0)

    jj = lax.broadcasted_iota(jnp.int32, (WIN, BQ), 0)
    ii = lax.broadcasted_iota(jnp.int32, (WIN, BQ), 1)

    def window_block(b, carry):
        base = pl.multiple_of(b * BQ, BQ)
        for h in range(n_heads):
            sc = jnp.dot(k_aug[pl.ds(base, BQ + 2 * WIN)], q_cols(qT, h, pl.ds(base, BQ), True), preferred_element_type=F32)
            sc = jnp.concatenate([jnp.where(ii <= jj, sc[:WIN], NEG), sc[WIN:WIN + BQ], jnp.where(jj <= ii, sc[WIN + BQ:], NEG)], axis=0)
            mx = jnp.max(sc, axis=0, keepdims=True)
            e = jnp.exp(sc - mx)
            m_w[b, pl.ds(h, 1)] = mx
            l_w[b, pl.ds(h, 1)] = jnp.sum(e, axis=0, keepdims=True)
            acc_w[b, pl.ds(h * hd, hd)] = jnp.dot(vT[pl.ds(h * hd, hd), pl.ds(base, BQ + 2 * WIN)], e.astype(BF16), preferred_element_type=F32)
        return carry

    lax.fori_loop(0, n_blk, window_block, 0)

    for c in ag:
        c.wait_recv()
    n_half = n_x * n_tp
    agd = remote(xg.at[pl.ds(core * n_half, n_half)], xg.at[pl.ds(core * n_half, n_half)], agd_s.at[0], agd_r.at[0], {'sp': partner})
    agd_in = remote(xg.at[pl.ds((1 - core) * n_half, n_half)], xg.at[pl.ds((1 - core) * n_half, n_half)], agd_s.at[0], agd_r.at[0], {'sp': partner})
    agd.start()
    for c in wy:
        c.wait_recv()
    for c in wf:
        c.start()
    agd_in.wait_recv()
    gb = BQ // per
    for g in range(G // BQ):
        rows = xg[pl.ds(g * gb, gb)].reshape(BQ, x_ref.shape[1])
        cols = pl.ds(g * BQ, BQ)
        project(rows, kg_aug, vgT, qgT, cols, cols, cols)

    gper = G // n_sp

    def gq_block(g, carry):
        cols = pl.ds(pl.multiple_of(g * BQ, BQ), BQ)
        for h in range(n_heads):
            sc = jnp.dot(k_aug[pl.ds(WIN, n_rows)], q_cols(qgT, h, cols, False), preferred_element_type=F32)
            mx = jnp.max(sc, axis=0, keepdims=True)
            e = jnp.exp(sc - mx)
            ls = jnp.sum(e, axis=0, keepdims=True)
            ac = jnp.dot(vT[pl.ds(h * hd, hd), pl.ds(WIN, n_rows)], e.astype(BF16), preferred_element_type=F32)
            for q in range(BQ // gper):
                cc = slice(q * gper, (q + 1) * gper)
                dst = g * (BQ // gper) + q
                part[dst, pl.ds(h * hd, hd)] = ac[:, cc]
                part[dst, pl.ds(width + h, 1)] = mx[:, cc]
                part[dst, pl.ds(width + 8 + h, 1)] = ls[:, cc]
        return carry

    lax.fori_loop(0, G // BQ, gq_block, 0)
    pt = [remote(part.at[sp(d)], part_recv.at[s], pt_s.at[d - 1], pt_r.at[d - 1], {'sp': sp(d)}) for d in range(1, n_sp)]
    for c in pt:
        c.start()
    for c in wf:
        c.wait_recv()
    for c in wx:
        c.start()
    wd[0].start()
    wd[1].start()

    def glob_block(b, carry):
        base = pl.multiple_of(b * BQ, BQ)
        for h in range(n_heads):
            sc = jnp.dot(kg_aug[...], q_cols(qT, h, pl.ds(base, BQ), False), preferred_element_type=F32)
            m_old = m_w[b, pl.ds(h, 1)]
            mx = jnp.maximum(jnp.max(sc, axis=0, keepdims=True), m_old)
            e = jnp.exp(sc - mx)
            alpha = jnp.exp(m_old - mx)
            ls = jnp.sum(e, axis=0, keepdims=True) + l_w[b, pl.ds(h, 1)] * alpha
            ac = jnp.dot(vgT[pl.ds(h * hd, hd)], e.astype(BF16), preferred_element_type=F32) + acc_w[b, pl.ds(h * hd, hd)] * alpha
            acc_w[b, pl.ds(h * hd, hd)] = ac / ls
        return carry

    lax.fori_loop(0, n_blk, glob_block, 0)

    for c in pt:
        c.wait_recv()
    part_recv[s] = part[s]
    for h in range(n_heads):
        ms = part_recv[:, pl.ds(width + h, 1)]
        mx = jnp.max(ms, axis=0, keepdims=True)
        wt = jnp.exp(ms - mx)
        den = jnp.sum(part_recv[:, pl.ds(width + 8 + h, 1)] * wt, axis=0)
        num = jnp.sum(part_recv[:, pl.ds(h * hd, hd)] * wt, axis=0)
        og_all[s, pl.ds(h * hd, hd)] = (num / den).astype(BF16)
    og = [remote(og_all.at[s], og_all.at[s], og_s.at[d - 1], og_r.at[d - 1], {'sp': sp(d)}) for d in range(1, n_sp)]
    for c in og:
        c.start()
    for c in og:
        c.wait_recv()
    og_ext[pl.ds(width, 16)] = jnp.ones((16, G), BF16)
    for d in range(n_sp):
        og_ext[pl.ds(0, width), pl.ds(d * gper, gper)] = og_all[d]

    chunk = n_rows // n_tp
    per_chunk = chunk // BQ
    gpos = gpos_ref[...]

    def pick_block(b, carry):
        pos = s * n_rows + b * BQ + lax.broadcasted_iota(jnp.int32, (BQ, G), 0)
        hot = (pos == gpos).astype(F32).astype(BF16)
        sel = lax.dot_general(og_ext[...], hot, NT, preferred_element_type=F32)
        res = jnp.where(sel[width:width + 1] > 0.5, sel[:width], acc_w[b])
        o_loc[b // per_chunk, :, pl.ds(pl.multiple_of((b % per_chunk) * BQ, BQ), BQ)] = res.astype(BF16)
        return carry

    lax.fori_loop(0, n_blk, pick_block, 0)
    a2a = [remote(o_loc.at[tp(-r)], o_ref.at[r], a2a_s.at[r - 1], a2a_r.at[r - 1], {'tp': tp(-r)}) for r in range(1, n_tp)]
    for c in a2a:
        c.start()
    own = pltpu.make_async_copy(o_loc.at[t], o_ref.at[0], loc_s)
    own.start()
    for c in wx_in:
        c.wait_recv()
    wd[2].start()
    wd[3].start()
    own.wait()
    for c in a2a:
        c.wait_recv()
    for c in wd_in:
        c.wait_recv()
    for c in rs + halo_c + ag + [agd] + pt + og + a2a + wy + wf + wx + wd:
        c.wait_send()


def mlp_kernel(dims, x_ref, o_ref, wcat_ref, wr_ref, y_ref,
               xbuf, wbuf, y_s, y_r, f_s, f_r, ld):
    n_sp, n_tp, n_heads, hd = dims
    n_rows, D = x_ref.shape
    width = n_heads * hd
    ff = (wcat_ref.shape[0] // 64) * 0 + D
    t = lax.axis_index('tp')

    def tp(d):
        return (t + d + n_tp) % n_tp

    chunk = n_rows // n_tp
    hrows = chunk // 2
    loads = [pltpu.make_async_copy(x_ref.at[pl.ds(pl.multiple_of(t * chunk, chunk), chunk)], xbuf, ld.at[n_tp]),
             pltpu.make_async_copy(wcat_ref, wbuf.at[0], ld.at[0])]
    for r in range(1, n_tp):
        loads.append(pltpu.make_async_copy(wr_ref.at[r - 1], wbuf.at[r], ld.at[r]))
    for c in loads:
        c.start()
    bar = pltpu.get_barrier_semaphore()
    for d in range(1, n_tp):
        pl.semaphore_signal(bar, inc=1, device_id={'tp': tp(d)}, device_id_type=MESH)
    pl.semaphore_wait(bar, n_tp - 1)
    for c in loads:
        c.wait()

    def rows_of(d, p):
        return pl.ds(pl.multiple_of(tp(d) * chunk + p * hrows, hrows), hrows)

    first, fwd, first_in, fwd_in = [], [], [], []
    for p in range(2):
        for j, d in enumerate((-1, 1)):
            first.append(remote(y_ref.at[rows_of(0, p)], y_ref.at[rows_of(0, p)], y_s.at[2 * p + j], y_r.at[2 * p + j], {'tp': tp(d)}))
            first_in.append(remote(y_ref.at[rows_of(-d, p)], y_ref.at[rows_of(-d, p)], y_s.at[2 * p + j], y_r.at[2 * p + j], {'tp': tp(d)}))
    fwd = [remote(y_ref.at[rows_of(1, 0)], y_ref.at[rows_of(1, 0)], f_s.at[0], f_r.at[0], {'tp': tp(-1)}),
           remote(y_ref.at[rows_of(-1, 1)], y_ref.at[rows_of(-1, 1)], f_s.at[1], f_r.at[1], {'tp': tp(1)})]
    fwd_in = [remote(y_ref.at[rows_of(2, 0)], y_ref.at[rows_of(2, 0)], f_s.at[0], f_r.at[0], {'tp': tp(-1)}),
              remote(y_ref.at[rows_of(2, 1)], y_ref.at[rows_of(2, 1)], f_s.at[1], f_r.at[1], {'tp': tp(1)})]

    for p in range(2):
        cols = pl.ds(p * hrows, hrows)
        mixed = jnp.zeros((hrows, D), F32)
        for r in range(n_tp):
            mixed = mixed + lax.dot_general(o_ref[r, :, cols], wbuf[r, pl.ds(2 * ff, width)], TN, preferred_element_type=F32)
        hidden = (xbuf[cols].astype(F32) + mixed).astype(BF16)
        down = jnp.zeros((hrows, D), F32)
        for r in range(n_tp):
            z = jnp.dot(hidden, wbuf[r, pl.ds(0, ff)], preferred_element_type=F32)
            u = jax.nn.gelu(z, approximate=True).astype(BF16)
            down = down + jnp.dot(u, wbuf[r, pl.ds(ff, ff)], preferred_element_type=F32)
        y_ref[rows_of(0, p)] = (hidden.astype(F32) + down).astype(BF16)
        first[2 * p].start()
        first[2 * p + 1].start()
    first_in[0].wait_recv()
    fwd[0].start()
    first_in[3].wait_recv()
    fwd[1].start()
    first_in[1].wait_recv()
    first_in[2].wait_recv()
    for c in fwd_in:
        c.wait_recv()
    for c in first + fwd:
        c.wait_send()


def solution(mesh):
    n_sp, n_tp = mesh.shape['sp'], mesh.shape['tp']

    def device_layer(tokens, glob_pos, w_query, w_key, w_value, w_out, w_up, w_down):
        n_rows, D = tokens.shape
        n_heads, hd = w_query.shape[1], w_query.shape[2]
        width = n_heads * hd
        G = glob_pos.shape[0]
        n_x = n_sp // 2
        per = G // (n_sp * n_tp)
        dims = (n_sp, n_tp, n_heads, hd)
        first = lax.axis_index('sp') * n_rows
        t = lax.axis_index('tp')
        ext_rows = n_rows + 2 * WIN

        slots = glob_pos.reshape(2, n_tp, n_x, per)
        slots = lax.dynamic_index_in_dim(slots, t, 1, keepdims=False).transpose(1, 0, 2).reshape(n_sp * per)
        hot = (slots[:, None] - first == jnp.arange(n_rows)[None, :]).astype(BF16)
        pick = jnp.dot(hot, tokens, preferred_element_type=F32).astype(BF16).reshape(n_sp, per, D)

        ext_pos = first - WIN + jnp.arange(ext_rows)
        off = jnp.any(ext_pos[:, None] == glob_pos[None, :], axis=1) | (ext_pos < 0) | (ext_pos >= n_rows * n_sp)
        kpad = jnp.where(off[:, None] & (jnp.arange(hd)[None, :] == 0), NEG, 0.0).astype(BF16)

        flat = lambda w: w.reshape(D, width)
        wqv = jnp.concatenate([flat(w_query).T, flat(w_value).T], axis=0)
        wtot = 2 * D + width
        wpad = -wtot % (n_sp * 16)
        wcat = jnp.concatenate([w_up, w_down, w_out.reshape(width, D), jnp.zeros((wpad, D), BF16)], axis=0)

        vm = pl.BlockSpec(memory_space=pltpu.VMEM)
        anyspace = pl.BlockSpec(memory_space=pl.ANY)
        dma = pltpu.SemaphoreType.DMA
        n_blk = n_rows // BQ
        o_all, wr = pl.pallas_call(
            functools.partial(attention_kernel, dims),
            out_shape=[jax.ShapeDtypeStruct((n_tp, width, n_rows // n_tp), BF16),
                       jax.ShapeDtypeStruct((n_tp - 1,) + wcat.shape, BF16)],
            in_specs=[vm] * 6 + [anyspace],
            out_specs=[vm, anyspace],
            scratch_shapes=[
                pltpu.VMEM((2, WIN, D), BF16), pltpu.VMEM((n_sp, per, D), BF16), pltpu.VMEM((n_sp * n_tp, per, D), BF16),
                pltpu.VMEM((width, n_rows), BF16), pltpu.VMEM((ext_rows, width + hd), BF16), pltpu.VMEM((width, ext_rows), BF16),
                pltpu.VMEM((width, G), BF16), pltpu.VMEM((G, width + hd), BF16), pltpu.VMEM((width, G), BF16),
                pltpu.VMEM((n_blk, 8, BQ), F32), pltpu.VMEM((n_blk, 8, BQ), F32), pltpu.VMEM((n_blk, width, BQ), F32),
                pltpu.VMEM((n_sp, width + 16, G // n_sp), F32), pltpu.VMEM((n_sp, width + 16, G // n_sp), F32),
                pltpu.VMEM((n_sp, width, G // n_sp), BF16), pltpu.VMEM((width + 16, G), BF16),
                pltpu.VMEM((n_tp, width, n_rows // n_tp), BF16),
                dma((2,)), dma((2,)), dma((n_sp - 1,)), dma((n_sp - 1,)), dma((n_x * n_tp - 1,)), dma((n_x * n_tp - 1,)),
                dma((1,)), dma((1,)), dma((n_sp - 1,)), dma((n_sp - 1,)), dma((n_sp - 1,)), dma((n_sp - 1,)),
                dma((n_tp - 1,)), dma((n_tp - 1,)), dma,
                dma((4,)), dma((4,)), dma((4,)), dma((4,)), dma((2,)), dma((2,)), dma((4,)), dma((4,)),
            ],
            compiler_params=pltpu.CompilerParams(collective_id=0, has_side_effects=True, vmem_limit_bytes=60 * 1024 * 1024),
            name='attention',
        )(tokens, pick, wqv, flat(w_key), kpad, glob_pos.reshape(1, G), wcat)

        return pl.pallas_call(
            functools.partial(mlp_kernel, dims),
            out_shape=jax.ShapeDtypeStruct((n_rows, D), BF16),
            in_specs=[anyspace, vm, anyspace, anyspace],
            out_specs=vm,
            scratch_shapes=[
                pltpu.VMEM((n_rows // n_tp, D), BF16), pltpu.VMEM((n_tp,) + wcat.shape, BF16),
                dma((4,)), dma((4,)), dma((2,)), dma((2,)), dma((n_tp + 1,)),
            ],
            compiler_params=pltpu.CompilerParams(collective_id=1, has_side_effects=True, vmem_limit_bytes=60 * 1024 * 1024),
            name='mlp',
        )(tokens, o_all, wcat, wr)

    row_spec = P(('dp', 'sp'), None)
    head_spec = P(None, 'tp', None)
    in_specs = (row_spec, P('dp'), head_spec, head_spec, head_spec, P('tp', None, None), P(None, 'tp'), P('tp', None))
    return jax.shard_map(device_layer, mesh=mesh, in_specs=in_specs, out_specs=row_spec, check_vma=False)
```

time: 691 us -> 173 us (0.25)
  waiting for transfers between devices: 300 us -> 0 us
  Pallas kernels: 0 us -> 151 us
  matrix products: 116 us -> 3.86 us
  local copies, waits for them, and re-layouts: 106 us -> 5.64 us
  blocking collectives: 77.7 us -> 0 us
  other arithmetic: 47.7 us -> 12.7 us
  between operations: 13.3 us -> 0.06 us
  starting transfers between devices: 12.3 us -> 0 us
  loops' own time: 11.8 us -> 0 us
    psum x3 -> x0, waiting for transfers between devices: 300 us -> none  [the longest x1 123 us: device_layer(): lax.psum(jnp.einsum('rhe,hed->rd', attn_rows, w_out, preferred_element_ty...]
    pallas_call x0 -> x2, Pallas kernels: none -> 151 us  [the longest x1 112 us: device_layer(): pl.pallas_call(functools.partial(attention_kernel, dims), out_shape=[jax....]
    dot_general x68 -> x1, matrix products: 108 us -> 3.86 us  [device_layer(): jnp.dot(hot, tokens, preferred_element_type=F32).astype(BF16)]
    psum x2 -> x0, blocking collectives: 54.1 us -> none  [the longest x1 30.4 us: global_queries(): return lax.psum(part_out, 'sp').astype(jnp.bfloat16)]
    scatter x1 -> x0, local copies, waits for them, and re-layouts: 48.9 us -> none  [device_layer(): attn_rows.at[jnp.where(owned, local_idx, n_rows)].set(glob_out, mode='drop')]
    gather x6 -> x0, local copies, waits for them, and re-layouts: 33.8 us -> none  [pick_rows(): picked = jnp.take(row_array, safe_idx, axis=0)]
    pmax x1 -> x0, blocking collectives: 23.6 us -> none  [global_queries(): glob_max = lax.pmax(jnp.max(scores, axis=2, keepdims=True), 'sp')]
    reduce_sum x33 -> x0, other arithmetic: 22 us -> none  [the longest x1 10.8 us: global_queries(): glob_sum = lax.psum(jnp.sum(exp_scores, axis=2, keepdims=True), 'sp')]
  transfers between devices with their start and end apart: 7 -> 0, of which waited for: 3 -> 0; matrix products, arithmetic and copies ran while one was open for 8% -> 0% of each run, Pallas kernels for 0% -> 0%
where the time goes in v1:
time: 173 us
  Pallas kernels  151 us (87%)
  other arithmetic  12.7 us (7%)
  local copies, waits for them, and re-layouts  5.64 us (3%)
  matrix products  3.86 us (2%)
    pallas_call x1, Pallas kernels, device_layer(): pl.pallas_call(functools.partial(attention_kernel, dims), out_shape=[jax....  112 us
    pallas_call x1, Pallas kernels, device_layer(): pl.pallas_call(functools.partial(mlp_kernel, dims), out_shape=jax.ShapeDt...  38.1 us
    concatenate x1, other arithmetic, device_layer(): jnp.concatenate([w_up, w_down, w_out.reshape(width, D), jnp.zeros((wpad,...  7.42 us
    dot_general x1, matrix products, device_layer(): jnp.dot(hot, tokens, preferred_element_type=F32).astype(BF16)  3.86 us
    unnamed x13, local copies, waits for them, and re-layouts  3.79 us

profile of v1, /device:TPU:97, one launch (start us, length us, event | category | flops | bytes accessed | tf_op | source)
XLA Modules:
  0.0 172.8 jit_solution(2009419892071980149)
XLA Ops:
  0.0 0.1 pad.3.clone
  0.1 2.3 %compare_reduce_fusion = pred[2560]{0:T(1024)(128)(4,1)S(1)} fusion(s32[1024]{0:T(1024)} %param.9, s32[2560]{0:T(1024)S(1)} %iota_add_fusion), kind=kLoop, calls=%fused_computation | loop fusion | flops 5240320 | bytes 16896 | tf_op jit(solution)/shard_map/reduce_or | solution.py:358
  2.4 0.8 reshape.48
  3.2 0.1 sub.27
  3.3 0.0 copy-start.3
  3.3 0.0 copy-start.4
  3.3 0.0 copy-start.5
  3.3 0.0 copy-start
  3.3 0.0 copy-start.1
  3.3 0.0 copy-start.2
  3.3 3.9 %fusion.1 = bf16[256,768]{1,0:T(8,128)(2,1)} fusion(bf16[2048,768]{1,0:T(8,128)(2,1)} %x_ref.3, s32[256]{0:T(256)S(1)} %sub.27), kind=kOutput, calls=%fused_computation.5 | convolution fusion | flops 806027264 | bytes 3539968 | tf_op jit(solution)/shard_map/dot_general | solution.py:355
  7.2 0.0 copy-done.3
  7.2 0.9 copy.14.wk_ref
  8.1 0.0 copy-done.4
  8.1 0.0 copy-done.5
  8.1 0.9 pad_maximum_fusion.wqv_ref
  9.0 2.1 %select_convert_fusion.kpad_ref = bf16[2560,64]{1,0:T(8,128)(2,1)} fusion(pred[64]{0:T(512)(128)(4,1)S(1)} %iota_compare_fusion.4, pred[2560]{0:T(1024)(128)(4,1)S(1)} %compare_or_fusion), kind=kLoop, calls=%fused_computation.4 | loop fusion | flops 491520 | bytes 330304 | tf_op jit(solution)/shard_map/convert_element_type | solution.py:359
  11.1 0.0 copy-done
  11.1 0.0 copy-done.1
  11.1 0.0 copy-done.2
  11.1 7.4 %maximum_maximum_fusion.wcat_ref = bf16[1792,768]{1,0:T(8,128)(2,1)} fusion(bf16[192,768]{1,0:T(8,128)(2,1)S(1)} %bitcast.16, bf16[768,768]{1,0:T(8,128)(2,1)S(1)} %copy-done, bf16[768,768]{1,0:T(8,128)(2,1)S(1)} %copy-done.1, bf16[1792]{0:T(1024)(128)(2,1)S(1)} %pad.3.clone), kind=kLoop, calls=%fused_computation.1 | loop fusion | flops 11010048 | bytes 5410304 | tf_op jit(solution)/shard_map/concatenate | solution.py:365
  18.5 112.5 %attention.1 = (bf16[4,192,512]{2,1,0:T(8,128)(2,1)}, bf16[3,1792,768]{2,1,0:T(8,128)(2,1)}) custom-call(bf16[2048,768]{1,0:T(8,128)(2,1)} %x_ref.3, bf16[8,32,768]{2,1,0:T(8,128)(2,1)} %bitcast.15, bf16[384,768]{1,0:T(8,128)(2,1)} %pad_maximum_fusion.wqv_ref, bf16[768,192]{1,0:T(8,128)(2,1)} %copy.14.wk_ref, bf16[2560,64]{1,0:T(8,128)(2,1)} %select_convert_fusion.kpad_ref, ...), custom_call_target="tpu_custom_call" | custom-call | tf_op jit(solution)/shard_map/attention/pallas_call | solution.py:371
  131.0 38.1 %mlp.1 = bf16[2048,768]{1,0:T(8,128)(2,1)} custom-call(bf16[2048,768]{1,0:T(8,128)(2,1)} %x_ref.3, bf16[4,192,512]{2,1,0:T(8,128)(2,1)} %get-tuple-element.7.o_ref, bf16[1792,768]{1,0:T(8,128)(2,1)} %maximum_maximum_fusion.wcat_ref, bf16[3,1792,768]{2,1,0:T(8,128)(2,1)} %get-tuple-element.8.wr_ref), custom_call_target="tpu_custom_call" | custom-call | tf_op jit(solution)/shard_map/mlp/pallas_call | solution.py:394
  169.1 3.8 %copy.16 = bf16[2048,768]{1,0:T(8,128)(2,1)} copy(bf16[2048,768]{1,0:T(8,128)(2,1)} %mlp.1) | data formatting | bytes 6291456
  (6 shorter events, 0.0 us)
Async XLA Ops:
  3.3 3.9 %copy-start.3 = (bf16[768,3,64]{0,2,1:T(8,128)(2,1)S(1)}, bf16[768,3,64]{0,2,1:T(8,128)(2,1)}, u32[]{:S(2)}) copy-start(bf16[768,3,64]{0,2,1:T(8,128)(2,1)} %param.11) | copy-start | bytes 884740
  3.3 4.8 %copy-start.4 = (bf16[768,3,64]{0,2,1:T(8,128)(2,1)S(1)}, bf16[768,3,64]{0,2,1:T(8,128)(2,1)}, u32[]{:S(2)}) copy-start(bf16[768,3,64]{0,2,1:T(8,128)(2,1)} %param.12) | copy-start | bytes 884740
  3.3 4.8 %copy-start.5 = (bf16[768,3,64]{0,2,1:T(8,128)(2,1)S(1)}, bf16[768,3,64]{0,2,1:T(8,128)(2,1)}, u32[]{:S(2)}) copy-start(bf16[768,3,64]{0,2,1:T(8,128)(2,1)} %param.10) | copy-start | bytes 884740
  3.3 7.8 %copy-start = (bf16[768,768]{1,0:T(8,128)(2,1)S(1)}, bf16[768,768]{1,0:T(8,128)(2,1)}, u32[]{:S(2)}) copy-start(bf16[768,768]{1,0:T(8,128)(2,1)} %param.15) | copy-start | bytes 3538948
  3.3 7.8 %copy-start.1 = (bf16[768,768]{1,0:T(8,128)(2,1)S(1)}, bf16[768,768]{1,0:T(8,128)(2,1)}, u32[]{:S(2)}) copy-start(bf16[768,768]{1,0:T(8,128)(2,1)} %param.14) | copy-start | bytes 3538948
  3.3 7.8 %copy-start.2 = (bf16[3,64,768]{2,1,0:T(8,128)(2,1)S(1)}, bf16[3,64,768]{2,1,0:T(8,128)(2,1)}, u32[]{:S(2)}) copy-start(bf16[3,64,768]{2,1,0:T(8,128)(2,1)} %param.13) | copy-start | bytes 884740

commit v2 on v1

v2 whole, which is shorter than its diff:
```python
import functools
import math

import jax
import jax.numpy as jnp
from jax import lax
from jax.experimental import pallas as pl
from jax.experimental.pallas import tpu as pltpu
from jax.sharding import PartitionSpec as P

WIN = 256
NEG = -1e38
LOG2E = math.log2(math.e)
BQ = 256
F32 = jnp.float32
BF16 = jnp.bfloat16
MESH = pl.DeviceIdType.MESH
NT = (((1,), (1,)), ((), ()))
TN = (((0,), (0,)), ((), ()))


def remote(src, dst, send, recv, where):
    return pltpu.make_async_remote_copy(src_ref=src, dst_ref=dst, send_sem=send, recv_sem=recv, device_id=where, device_id_type=MESH)


def layer_kernel(dims, x_ref, wqv_ref, wk_ref, scol_ref, gpos_ref, w1_ref, w2_ref, wo_ref,
                 y_ref,
                 w1_in, w2_in, wo_in, pick, halo, rs_recv, xg, s_scr, m_scr, qT, k_aug, vT, qgT, kg_aug, vgT, m_w, l_w, acc_w, part, part_recv,
                 og_all, og_ext, o_loc, o_in,
                 halo_s, halo_r, rs_s, rs_r, ag_s, ag_r, agd_s, agd_r, pt_s, pt_r, og_s, og_r, a2a_s, a2a_r,
                 wy_s, wy_r, wf_s, wf_r, wx_s, wx_r, wd_s, wd_r, y_s, y_r, f_s, f_r):
    n_sp, n_tp, n_heads, hd = dims
    n_rows, D = x_ref.shape
    width = n_heads * hd
    n_x = n_sp // 2
    n_blk = n_rows // BQ
    s = lax.axis_index('sp')
    t = lax.axis_index('tp')
    core = s % 2
    chip = s // 2
    G = gpos_ref.shape[1]
    per = G // (n_sp * n_tp)
    wrows = D // n_sp

    def sp(d):
        return (s + d + n_sp) % n_sp

    def tp(d):
        return (t + d + n_tp) % n_tp

    bar = pltpu.get_barrier_semaphore()
    n_peers = 0
    for d in range(1, n_sp):
        pl.semaphore_signal(bar, inc=1, device_id={'sp': sp(d)}, device_id_type=MESH)
        n_peers += 1
    for dt in range(1, n_tp):
        for dx in range(n_x):
            pl.semaphore_signal(bar, inc=1, device_id={'sp': sp(2 * dx), 'tp': tp(dt)}, device_id_type=MESH)
            n_peers += 1
    pl.semaphore_wait(bar, n_peers)

    halo_c = [remote(x_ref.at[pl.ds(n_rows - WIN, WIN)], halo.at[0], halo_s.at[0], halo_r.at[0], {'sp': sp(1)}),
              remote(x_ref.at[pl.ds(0, WIN)], halo.at[1], halo_s.at[1], halo_r.at[1], {'sp': sp(-1)})]
    for c in halo_c:
        c.start()

    weights = [(w1_ref, w1_in), (wo_ref, wo_in), (w2_ref, w2_in)]

    def wslice(piece):
        return pl.ds(pl.multiple_of(((piece + n_sp) % n_sp) * wrows, wrows), wrows)

    wy, wf, wx, wx_in, wd, wd_in = [], [], [], [], [], []
    partner = 2 * chip + 1 - core
    for p in range(2):
        rows = wslice(s + 2 * p)
        wy.append([remote(w.at[rows], win.at[slot, rows], wy_s.at[p, k, a], wy_r.at[p, k, a], {'tp': tp(d)})
                   for k, (d, slot) in enumerate(((-1, 0), (1, 2))) for a, (w, win) in enumerate(weights)])
        wf.append([remote(win.at[slot, rows], win.at[1, rows], wf_s.at[p, a], wf_r.at[p, a], {'tp': tp(d)})
                   for a, ((w, win), slot, d) in enumerate(zip(weights, (0, 0, 2), (-1, -1, 1)))])
        come = wslice(s - 2 if p == 0 else s + 4)
        wx.append([remote(win.at[:, rows], win.at[:, rows], wx_s.at[p, a], wx_r.at[p, a], {'sp': sp(2 - 4 * p)}) for a, (w, win) in enumerate(weights)])
        wx_in.append([remote(win.at[:, come], win.at[:, come], wx_s.at[p, a], wx_r.at[p, a], {'sp': sp(2 - 4 * p)}) for a, (w, win) in enumerate(weights)])
    for j in range(4):
        rows, come = wslice(s + 2 * j), wslice(partner + 2 * j)
        wd.append([remote(win.at[:, rows], win.at[:, rows], wd_s.at[j, a], wd_r.at[j, a], {'sp': partner}) for a, (w, win) in enumerate(weights)])
        wd_in.append([remote(win.at[:, come], win.at[:, come], wd_s.at[j, a], wd_r.at[j, a], {'sp': partner}) for a, (w, win) in enumerate(weights)])

    def start(copies):
        for c in copies:
            c.start()

    def arrive(copies):
        for c in copies:
            c.wait_recv()

    start(wy[0])

    hot = (s * n_rows + lax.broadcasted_iota(jnp.int32, (n_sp * per, n_rows), 1) == scol_ref[...]).astype(F32).astype(BF16)
    pick[...] = jnp.dot(hot, x_ref[...], preferred_element_type=F32).astype(BF16).reshape(n_sp, per, D)

    rs = [remote(pick.at[sp(d)], rs_recv.at[s], rs_s.at[d - 1], rs_r.at[d - 1], {'sp': sp(d)}) for d in range(1, n_sp)]
    start(rs)

    def project(rows, pad, kdst, vdst, qdst, kdst_row, vcol, qcol):
        qv = lax.dot_general(wqv_ref[...], rows, NT, preferred_element_type=F32).astype(BF16)
        kk = jnp.dot(rows, wk_ref[...], preferred_element_type=F32).astype(BF16)
        vdst[:, vcol] = qv[width:]
        for h in range(n_heads):
            kh = kk[:, h * hd:(h + 1) * hd]
            kdst[h, kdst_row, pl.ds(0, 2 * hd)] = jnp.concatenate([kh, kh], axis=1)
            kdst[h, kdst_row, pl.ds(2 * hd, 2 * hd)] = jnp.concatenate([kh, pad], axis=1)
        if qdst is not None:
            rest = qv[:width].astype(F32) * (LOG2E / math.sqrt(hd))
            for i in range(3):
                cut = rest.astype(BF16)
                rest = rest - cut.astype(F32)
                for h in range(n_heads):
                    qdst[h, pl.ds(i * hd, hd), qcol] = cut[h * hd:(h + 1) * hd]

    gpos = gpos_ref[...]
    mark = jnp.where(lax.broadcasted_iota(jnp.int32, (G, hd), 1) == 0, NEG, 0.0).astype(BF16)

    def key_pad(off):
        pos = s * n_rows + off + lax.broadcasted_iota(jnp.int32, (BQ, G), 0)
        pad = jnp.dot((pos == gpos).astype(F32).astype(BF16), mark, preferred_element_type=F32)
        at = s * n_rows + off + lax.broadcasted_iota(jnp.int32, (BQ, hd), 0)
        lane = lax.broadcasted_iota(jnp.int32, (BQ, hd), 1)
        return jnp.where((lane == 0) & ((at < 0) | (at >= n_rows * n_sp)), NEG, pad).astype(BF16)

    def proj_block(b, carry):
        base = pl.multiple_of(b * BQ, BQ)
        ext = pl.multiple_of(b * BQ + WIN, BQ)
        project(x_ref[pl.ds(base, BQ)], key_pad(base), k_aug, vT, qT, pl.ds(ext, BQ), pl.ds(ext, BQ), pl.ds(base, BQ))
        return carry

    flag_row = (lax.broadcasted_iota(jnp.int32, (hd, BQ), 0) == 0).astype(F32).astype(BF16)
    for h in range(n_heads):
        for b in range(n_blk):
            qT[h, pl.ds(3 * hd, hd), pl.ds(b * BQ, BQ)] = flag_row
        qgT[h, pl.ds(3 * hd, hd)] = jnp.zeros((hd, G), BF16)
    lax.fori_loop(0, n_blk, proj_block, 0)

    for c in rs:
        c.wait_recv()
    mine = core * (n_x * n_tp) + t * n_x + chip
    rs_recv[s] = pick[s]
    xg[mine] = jnp.sum(rs_recv[...].astype(F32), axis=0).astype(BF16)
    ag = []
    for dt in range(n_tp):
        for dx in range(n_x):
            if dt or dx:
                j = dt * n_x + dx - 1
                ag.append(remote(xg.at[mine], xg.at[mine], ag_s.at[j], ag_r.at[j], {'sp': sp(2 * dx), 'tp': tp(dt)}))
    start(ag)
    arrive(wy[0])
    start(wf[0])
    start(wy[1])
    arrive(halo_c)
    project(halo[0], key_pad(-WIN), k_aug, vT, None, pl.ds(0, WIN), pl.ds(0, WIN), None)
    project(halo[1], key_pad(n_rows), k_aug, vT, None, pl.ds(n_rows + WIN, WIN), pl.ds(n_rows + WIN, WIN), None)

    jj = lax.broadcasted_iota(jnp.int32, (WIN, BQ), 0)
    ii = lax.broadcasted_iota(jnp.int32, (WIN, BQ), 1)

    def pipeline(n_blocks, n_ch, keys, queries, values, window, finish):
        def score(b, h, c, mx):
            sc = jnp.dot(keys(b, h, c), queries(b, h), preferred_element_type=F32)
            if window and c == 0:
                sc = jnp.where(ii <= jj, sc, NEG)
            if window and c == n_ch - 1:
                sc = jnp.where(jj <= ii, sc, NEG)
            s_scr[h, pl.ds(c * BQ, BQ)] = sc
            top = jnp.max(sc.reshape(BQ // 8, 8, BQ), axis=0)
            return top if mx is None else jnp.maximum(mx, top)

        def first(b, h):
            mx = None
            for c in range(n_ch):
                mx = score(b, h, c, mx)
            m_scr[h] = mx

        def both(b, h, b2, h2):
            mx = jnp.max(m_scr[h], axis=0, keepdims=True)
            mx = finish(b, h, mx, None, None, True)
            nxt, ls, ac = None, None, None
            for c in range(n_ch):
                nxt = score(b2, h2, c, nxt)
                e = jnp.exp2(s_scr[h, pl.ds(c * BQ, BQ)] - mx)
                le = jnp.sum(e.reshape(BQ // 8, 8, BQ), axis=0)
                ls = le if ls is None else ls + le
                pv = jnp.dot(values(b, h, c), e.astype(BF16), preferred_element_type=F32)
                ac = pv if ac is None else ac + pv
            m_scr[h2] = nxt
            finish(b, h, mx, jnp.sum(ls, axis=0, keepdims=True), ac, False)

        def body(b, carry):
            for h in range(n_heads):
                if h + 1 < n_heads:
                    both(b, h, b, h + 1)
                else:
                    both(b, h, jnp.minimum(b + 1, n_blocks - 1), 0)
            return carry

        first(0, 0)
        lax.fori_loop(0, n_blocks, body, 0)

    def cols_of(b):
        return pl.ds(pl.multiple_of(b * BQ, BQ), BQ)

    def rows_at(b, c, off=0):
        return pl.ds(pl.multiple_of(b * BQ + c * BQ + off, BQ), BQ)

    def window_done(b, h, mx, ls, ac, start):
        if start:
            return mx
        m_w[b, pl.ds(h, 1)] = mx
        l_w[b, pl.ds(h, 1)] = ls
        acc_w[b, pl.ds(h * hd, hd)] = ac

    pipeline(n_blk, 1 + 2 * WIN // BQ, lambda b, h, c: k_aug[h, rows_at(b, c)], lambda b, h: qT[h, :, cols_of(b)],
             lambda b, h, c: vT[pl.ds(h * hd, hd), rows_at(b, c)], True, window_done)

    for c in ag:
        c.wait_recv()
    n_half = n_x * n_tp
    agd = remote(xg.at[pl.ds(core * n_half, n_half)], xg.at[pl.ds(core * n_half, n_half)], agd_s.at[0], agd_r.at[0], {'sp': partner})
    agd_in = remote(xg.at[pl.ds((1 - core) * n_half, n_half)], xg.at[pl.ds((1 - core) * n_half, n_half)], agd_s.at[0], agd_r.at[0], {'sp': partner})
    agd.start()
    arrive(wf[0])
    start(wx[0])
    arrive(wy[1])
    start(wf[1])
    agd_in.wait_recv()
    gb = BQ // per
    for g in range(G // BQ):
        rows = xg[pl.ds(g * gb, gb)].reshape(BQ, x_ref.shape[1])
        cols = pl.ds(g * BQ, BQ)
        project(rows, jnp.zeros((BQ, hd), BF16), kg_aug, vgT, qgT, cols, cols, cols)

    gper = G // n_sp

    def gq_done(g, h, mx, ls, ac, start):
        if start:
            return mx
        for q in range(BQ // gper):
            cc = slice(q * gper, (q + 1) * gper)
            dst = g * (BQ // gper) + q
            part[dst, pl.ds(h * hd, hd)] = ac[:, cc]
            part[dst, pl.ds(width + h, 1)] = mx[:, cc]
            part[dst, pl.ds(width + 8 + h, 1)] = ls[:, cc]

    pipeline(G // BQ, n_rows // BQ, lambda b, h, c: k_aug[h, pl.ds(WIN + c * BQ, BQ)], lambda b, h: qgT[h, :, cols_of(b)],
             lambda b, h, c: vT[pl.ds(h * hd, hd), pl.ds(WIN + c * BQ, BQ)], False, gq_done)
    pt = [remote(part.at[sp(d)], part_recv.at[s], pt_s.at[d - 1], pt_r.at[d - 1], {'sp': sp(d)}) for d in range(1, n_sp)]
    for c in pt:
        c.start()
    arrive(wf[1])
    start(wx[1])
    start(wd[0])
    start(wd[1])

    def glob_done(b, h, mx, ls, ac, start):
        m_old = m_w[b, pl.ds(h, 1)]
        if start:
            return jnp.maximum(mx, m_old)
        alpha = jnp.exp2(m_old - mx)
        total = ls + l_w[b, pl.ds(h, 1)] * alpha
        acc_w[b, pl.ds(h * hd, hd)] = (ac + acc_w[b, pl.ds(h * hd, hd)] * alpha) / total

    pipeline(n_blk, G // BQ, lambda b, h, c: kg_aug[h, pl.ds(c * BQ, BQ)], lambda b, h: qT[h, :, cols_of(b)],
             lambda b, h, c: vgT[pl.ds(h * hd, hd), pl.ds(c * BQ, BQ)], False, glob_done)

    for c in pt:
        c.wait_recv()
    part_recv[s] = part[s]
    for h in range(n_heads):
        ms = part_recv[:, pl.ds(width + h, 1)]
        mx = jnp.max(ms, axis=0, keepdims=True)
        wt = jnp.exp2(ms - mx)
        den = jnp.sum(part_recv[:, pl.ds(width + 8 + h, 1)] * wt, axis=0)
        num = jnp.sum(part_recv[:, pl.ds(h * hd, hd)] * wt, axis=0)
        og_all[s, pl.ds(h * hd, hd)] = (num / den).astype(BF16)
    og = [remote(og_all.at[s], og_all.at[s], og_s.at[d - 1], og_r.at[d - 1], {'sp': sp(d)}) for d in range(1, n_sp)]
    for c in og:
        c.start()
    for c in og:
        c.wait_recv()
    og_ext[pl.ds(width, 16)] = jnp.ones((16, G), BF16)
    for d in range(n_sp):
        og_ext[pl.ds(0, width), pl.ds(d * gper, gper)] = og_all[d]

    chunk = n_rows // n_tp
    per_chunk = chunk // BQ
    a2a = []
    for p in range(per_chunk):
        def pick_block(ch, carry):
            b = ch * per_chunk + p
            pos = s * n_rows + b * BQ + lax.broadcasted_iota(jnp.int32, (BQ, G), 0)
            hot = (pos == gpos).astype(F32).astype(BF16)
            sel = lax.dot_general(og_ext[...], hot, NT, preferred_element_type=F32)
            o_loc[p, ch] = jnp.where(sel[width:width + 1] > 0.5, sel[:width], acc_w[b]).astype(BF16)
            return carry

        lax.fori_loop(0, n_tp, pick_block, 0)
        a2a.append([remote(o_loc.at[p, tp(-r)], o_in.at[p, r - 1], a2a_s.at[p, r - 1], a2a_r.at[p, r - 1], {'tp': tp(-r)}) for r in range(1, n_tp)])
        start(a2a[p])
    arrive(wx_in[0])
    start(wd[3])
    arrive(wx_in[1])
    start(wd[2])

    def rows_of(d, p):
        return pl.ds(pl.multiple_of(tp(d) * chunk + p * BQ, BQ), BQ)

    first, first_in = [], []
    for p in range(2):
        for j, d in enumerate((-1, 1)):
            first.append(remote(y_ref.at[rows_of(0, p)], y_ref.at[rows_of(0, p)], y_s.at[2 * p + j], y_r.at[2 * p + j], {'tp': tp(d)}))
            first_in.append(remote(y_ref.at[rows_of(-d, p)], y_ref.at[rows_of(-d, p)], y_s.at[2 * p + j], y_r.at[2 * p + j], {'tp': tp(d)}))
    fwd = [remote(y_ref.at[rows_of(1, 0)], y_ref.at[rows_of(1, 0)], f_s.at[0], f_r.at[0], {'tp': tp(-1)}),
           remote(y_ref.at[rows_of(-1, 1)], y_ref.at[rows_of(-1, 1)], f_s.at[1], f_r.at[1], {'tp': tp(1)})]
    fwd_in = [remote(y_ref.at[rows_of(2, 0)], y_ref.at[rows_of(2, 0)], f_s.at[0], f_r.at[0], {'tp': tp(-1)}),
              remote(y_ref.at[rows_of(2, 1)], y_ref.at[rows_of(2, 1)], f_s.at[1], f_r.at[1], {'tp': tp(1)})]

    for p in range(2):
        arrive(a2a[p])
        if p == 0:
            for group in wd_in:
                arrive(group)
        mixed = jnp.zeros((BQ, D), F32)
        for r in range(n_tp):
            o_r = o_loc[p, t] if r == 0 else o_in[p, r - 1]
            w = wo_ref[...] if r == 0 else wo_in[r - 1]
            mixed = mixed + lax.dot_general(o_r, w, (((0,), (1,)), ((), ())), preferred_element_type=F32)
        hidden = (x_ref[rows_of(0, p)].astype(F32) + mixed).astype(BF16)
        down = jnp.zeros((BQ, D), F32)
        for r in range(n_tp):
            z = jnp.dot(hidden, w1_ref[...] if r == 0 else w1_in[r - 1], preferred_element_type=F32)
            u = jax.nn.gelu(z, approximate=True).astype(BF16)
            down = down + jnp.dot(u, w2_ref[...] if r == 0 else w2_in[r - 1], preferred_element_type=F32)
        y_ref[rows_of(0, p)] = (hidden.astype(F32) + down).astype(BF16)
        first[2 * p].start()
        first[2 * p + 1].start()
    first_in[0].wait_recv()
    fwd[0].start()
    first_in[3].wait_recv()
    fwd[1].start()
    first_in[1].wait_recv()
    first_in[2].wait_recv()
    arrive(fwd_in)
    for c in rs + halo_c + ag + [agd] + pt + og + sum(a2a + wy + wf + wx + wd, []) + first + fwd:
        c.wait_send()


def solution(mesh):
    n_sp, n_tp = mesh.shape['sp'], mesh.shape['tp']

    def device_layer(tokens, glob_pos, w_query, w_key, w_value, w_out, w_up, w_down):
        n_rows, D = tokens.shape
        n_heads, hd = w_query.shape[1], w_query.shape[2]
        width = n_heads * hd
        G = glob_pos.shape[0]
        n_x = n_sp // 2
        per = G // (n_sp * n_tp)
        dims = (n_sp, n_tp, n_heads, hd)
        t = lax.axis_index('tp')
        ext_rows = n_rows + 2 * WIN

        slots = glob_pos.reshape(2, n_tp, n_x, per)
        slots = lax.dynamic_index_in_dim(slots, t, 1, keepdims=False).transpose(1, 0, 2).reshape(n_sp * per)
        flat = lambda w: w.reshape(D, width)
        wqv = jnp.concatenate([flat(w_query).T, flat(w_value).T], axis=0)
        vm = pl.BlockSpec(memory_space=pltpu.VMEM)
        dma = pltpu.SemaphoreType.DMA
        n_blk = n_rows // BQ
        return pl.pallas_call(
            functools.partial(layer_kernel, dims),
            out_shape=jax.ShapeDtypeStruct((n_rows, D), BF16),
            in_specs=[vm] * 8,
            out_specs=vm,
            scratch_shapes=[
                pltpu.VMEM((n_tp - 1,) + w_up.shape, BF16), pltpu.VMEM((n_tp - 1,) + w_down.shape, BF16), pltpu.VMEM((n_tp - 1, D, width), BF16),
                pltpu.VMEM((n_sp, per, D), BF16),
                pltpu.VMEM((2, WIN, D), BF16), pltpu.VMEM((n_sp, per, D), BF16), pltpu.VMEM((n_sp * n_tp, per, D), BF16),
                pltpu.VMEM((n_heads, n_rows, BQ), F32), pltpu.VMEM((n_heads, 8, BQ), F32),
                pltpu.VMEM((n_heads, 4 * hd, n_rows), BF16), pltpu.VMEM((n_heads, ext_rows, 4 * hd), BF16), pltpu.VMEM((width, ext_rows), BF16),
                pltpu.VMEM((n_heads, 4 * hd, G), BF16), pltpu.VMEM((n_heads, G, 4 * hd), BF16), pltpu.VMEM((width, G), BF16),
                pltpu.VMEM((n_blk, 8, BQ), F32), pltpu.VMEM((n_blk, 8, BQ), F32), pltpu.VMEM((n_blk, width, BQ), F32),
                pltpu.VMEM((n_sp, width + 16, G // n_sp), F32), pltpu.VMEM((n_sp, width + 16, G // n_sp), F32),
                pltpu.VMEM((n_sp, width, G // n_sp), BF16), pltpu.VMEM((width + 16, G), BF16),
                pltpu.VMEM((2, n_tp, width, BQ), BF16), pltpu.VMEM((2, n_tp - 1, width, BQ), BF16),
                dma((2,)), dma((2,)), dma((n_sp - 1,)), dma((n_sp - 1,)), dma((n_x * n_tp - 1,)), dma((n_x * n_tp - 1,)),
                dma((1,)), dma((1,)), dma((n_sp - 1,)), dma((n_sp - 1,)), dma((n_sp - 1,)), dma((n_sp - 1,)),
                dma((2, n_tp - 1)), dma((2, n_tp - 1)),
                dma((2, 2, 3)), dma((2, 2, 3)), dma((2, 3)), dma((2, 3)), dma((2, 3)), dma((2, 3)), dma((4, 3)), dma((4, 3)),
                dma((4,)), dma((4,)), dma((2,)), dma((2,)),
            ],
            compiler_params=pltpu.CompilerParams(collective_id=0, has_side_effects=True, vmem_limit_bytes=62 * 1024 * 1024),
            name='layer',
        )(tokens, wqv, flat(w_key), slots.reshape(-1, 1), glob_pos.reshape(1, G), w_up, w_down, w_out.reshape(width, D).T)

    row_spec = P(('dp', 'sp'), None)
    head_spec = P(None, 'tp', None)
    in_specs = (row_spec, P('dp'), head_spec, head_spec, head_spec, P('tp', None, None), P(None, 'tp'), P('tp', None))
    return jax.shard_map(device_layer, mesh=mesh, in_specs=in_specs, out_specs=row_spec, check_vma=False)
```

time: 173 us -> 141 us (0.82)
  Pallas kernels: 151 us -> 130 us
  other arithmetic: 12.7 us -> 0.85 us
  matrix products: 3.86 us -> 0 us
  local copies, waits for them, and re-layouts: 5.64 us -> 9.14 us
    pallas_call x2 -> x1, Pallas kernels: 151 us -> 130 us  [device_layer(): pl.pallas_call(functools.partial(layer_kernel, dims), out_shape=jax.Shape...]
    concatenate x1 -> x0, other arithmetic: 7.42 us -> none  [device_layer(): jnp.concatenate([w_up, w_down, w_out.reshape(width, D), jnp.zeros((wpad,...]
    dot_general x1 -> x0, matrix products: 3.86 us -> none  [device_layer(): jnp.dot(hot, tokens, preferred_element_type=F32).astype(BF16)]
    reduce_or x1 -> x0, other arithmetic: 2.3 us -> none  [device_layer(): jnp.any(ext_pos[:, None] == glob_pos[None, :], axis=1) | (ext_pos < 0)]
    convert_element_type x1 -> x0, other arithmetic: 2.06 us -> none  [device_layer(): jnp.where(off[:, None] & (jnp.arange(hd)[None, :] == 0), NEG, 0.0)]
    reshape x0 -> x1, local copies, waits for them, and re-layouts: none -> 1.87 us  [device_layer(): w_out.reshape(width, D)]
    unnamed x13 -> x5, local copies, waits for them, and re-layouts: 3.79 us -> 3.76 us
where the time goes in v2:
time: 141 us; the launch traced here: 140 us
  Pallas kernels  130 us (92%)
  local copies, waits for them, and re-layouts  9.14 us (6%)
    pallas_call x1, Pallas kernels, device_layer(): pl.pallas_call(functools.partial(layer_kernel, dims), out_shape=jax.Shape...  130 us
    unnamed x5, local copies, waits for them, and re-layouts  3.76 us

profile of v2, /device:TPU:97, one launch (start us, length us, event | category | flops | bytes accessed | tf_op | source)
XLA Modules:
  0.0 140.3 jit_solution(8031228578490487876)
XLA Ops:
  0.0 0.0 copy-start
  0.0 0.0 copy-start.1
  0.0 0.8 reshape.21
  0.8 0.8 reshape_reshape.4.scol_ref
  1.6 1.9 %copy.16.wk_ref = bf16[768,192]{1,0:T(8,128)(2,1)} copy(bf16[768,192]{0,1:T(8,128)(2,1)} %bitcast.15) | data formatting | bytes 589824 | tf_op jit(solution)/shard_map/reshape | solution.py:371
  3.5 1.9 %copy.15 = bf16[192,768]{0,1:T(8,128)(2,1)} copy(bf16[192,768]{1,0:T(8,128)(2,1)} %bitcast.16) | data formatting | bytes 589824 | tf_op jit(solution)/shard_map/reshape | solution.py:400
  5.4 0.0 copy-done
  5.4 0.0 copy-done.1
  5.4 0.9 pad_maximum_fusion.wqv_ref
  6.2 130.3 %layer.1 = bf16[2048,768]{1,0:T(8,128)(2,1)} custom-call(bf16[2048,768]{1,0:T(8,128)(2,1)} %x_ref.1, bf16[384,768]{1,0:T(8,128)(2,1)} %pad_maximum_fusion.wqv_ref, bf16[768,192]{1,0:T(8,128)(2,1)} %copy.16.wk_ref, s32[256,1]{1,0:T(8,128)} %reshape_reshape.4.scol_ref, s32[1,1024]{1,0:T(1,128)} %bitcast.19, bf16[768,768]{1,0:T(8,128)(2,1)} %w1_ref.1, ...), custom_call_target="tpu_custom_call" | custom-call | tf_op jit(solution)/shard_map/layer/pallas_call | solution.py:376
  136.5 3.8 %copy.19 = bf16[2048,768]{1,0:T(8,128)(2,1)} copy(bf16[2048,768]{1,0:T(8,128)(2,1)} %layer.1) | data formatting | bytes 6291456
  (2 shorter events, 0.0 us)
Async XLA Ops:
  0.0 5.4 %copy-start = (bf16[768,3,64]{0,2,1:T(8,128)(2,1)S(1)}, bf16[768,3,64]{0,2,1:T(8,128)(2,1)}, u32[]{:S(2)}) copy-start(bf16[768,3,64]{0,2,1:T(8,128)(2,1)} %param.12) | copy-start | bytes 884740
  0.0 5.4 %copy-start.1 = (bf16[768,3,64]{0,2,1:T(8,128)(2,1)S(1)}, bf16[768,3,64]{0,2,1:T(8,128)(2,1)}, u32[]{:S(2)}) copy-start(bf16[768,3,64]{0,2,1:T(8,128)(2,1)} %param.10) | copy-start | bytes 884740

commit v3 on v2

--- a/solution.py
+++ b/solution.py
@@ -23,12 +23,12 @@
     return pltpu.make_async_remote_copy(src_ref=src, dst_ref=dst, send_sem=send, recv_sem=recv, device_id=where, device_id_type=MESH)
 
 
-def layer_kernel(dims, x_ref, wqv_ref, wk_ref, scol_ref, gpos_ref, w1_ref, w2_ref, wo_ref,
+def layer_kernel(dims, x_ref, wqv_ref, wk_ref, gpos_ref, w1_ref, w2_ref, wo_ref,
                  y_ref,
-                 w1_in, w2_in, wo_in, pick, halo, rs_recv, xg, s_scr, m_scr, qT, k_aug, vT, qgT, kg_aug, vgT, m_w, l_w, acc_w, part, part_recv,
+                 w1_own, w2_own, wo_own, w1_in, w2_in, wo_in, pick, halo, rs_recv, xg, s_scr, m_scr, qT, k_aug, vT, qgT, kg_aug, vgT, m_w, l_w, acc_w, part, part_recv,
                  og_all, og_ext, o_loc, o_in,
                  halo_s, halo_r, rs_s, rs_r, ag_s, ag_r, agd_s, agd_r, pt_s, pt_r, og_s, og_r, a2a_s, a2a_r,
-                 wy_s, wy_r, wf_s, wf_r, wx_s, wx_r, wd_s, wd_r, y_s, y_r, f_s, f_r):
+                 wy_s, wy_r, wf_s, wf_r, wx_s, wx_r, wd_s, wd_r, y_s, y_r, f_s, f_r, own_s):
     n_sp, n_tp, n_heads, hd = dims
     n_rows, D = x_ref.shape
     width = n_heads * hd
@@ -38,15 +38,18 @@
     t = lax.axis_index('tp')
     core = s % 2
     chip = s // 2
-    G = gpos_ref.shape[1]
+    G = gpos_ref.shape[0] * gpos_ref.shape[1]
+    gpos = jnp.concatenate([gpos_ref[pl.ds(i, 1)] for i in range(gpos_ref.shape[0])], axis=1)
     per = G // (n_sp * n_tp)
-    wrows = D // n_sp
-
     def sp(d):
         return (s + d + n_sp) % n_sp
 
     def tp(d):
         return (t + d + n_tp) % n_tp
+
+    own = [pltpu.make_async_copy(a, b, own_s.at[i]) for i, (a, b) in enumerate(((wo_ref, wo_own), (w1_ref, w1_own), (w2_ref, w2_own)))]
+    for c in own:
+        c.start()
 
     bar = pltpu.get_barrier_semaphore()
     n_peers = 0
@@ -64,26 +67,41 @@
     for c in halo_c:
         c.start()
 
-    weights = [(w1_ref, w1_in), (wo_ref, wo_in), (w2_ref, w2_in)]
-
-    def wslice(piece):
-        return pl.ds(pl.multiple_of(((piece + n_sp) % n_sp) * wrows, wrows), wrows)
-
-    wy, wf, wx, wx_in, wd, wd_in = [], [], [], [], [], []
+    weights = [(wo_ref, wo_in, 2 * width // n_sp, 2), (w1_ref, w1_in, D // n_sp, 1), (w2_ref, w2_in, D // n_sp, 1)]
+
+    def wslice(piece, size, share):
+        return pl.ds(pl.multiple_of((((piece + n_sp) % n_sp) // share) * size, size), size)
+
+    wy, wf, wxa, wxa_in, wxb, wxb_in, wd, wd_in = [], [], [], [], [], [], [], []
     partner = 2 * chip + 1 - core
     for p in range(2):
-        rows = wslice(s + 2 * p)
-        wy.append([remote(w.at[rows], win.at[slot, rows], wy_s.at[p, k, a], wy_r.at[p, k, a], {'tp': tp(d)})
-                   for k, (d, slot) in enumerate(((-1, 0), (1, 2))) for a, (w, win) in enumerate(weights)])
-        wf.append([remote(win.at[slot, rows], win.at[1, rows], wf_s.at[p, a], wf_r.at[p, a], {'tp': tp(d)})
-                   for a, ((w, win), slot, d) in enumerate(zip(weights, (0, 0, 2), (-1, -1, 1)))])
-        come = wslice(s - 2 if p == 0 else s + 4)
-        wx.append([remote(win.at[:, rows], win.at[:, rows], wx_s.at[p, a], wx_r.at[p, a], {'sp': sp(2 - 4 * p)}) for a, (w, win) in enumerate(weights)])
-        wx_in.append([remote(win.at[:, come], win.at[:, come], wx_s.at[p, a], wx_r.at[p, a], {'sp': sp(2 - 4 * p)}) for a, (w, win) in enumerate(weights)])
+        gy, gf, ga, ga_in, gb2, gb_in = [], [], [], [], [], []
+        d2 = {'sp': sp(2 - 4 * p)}
+        for a, (w, win, size, share) in enumerate(weights):
+            rows = wslice(s + 2 * p, size, share)
+            come = wslice(s - 2 if p == 0 else s + 4, size, share)
+            for k, (d, slot) in enumerate(((-1, 0), (1, 2))):
+                gy.append(remote(w.at[rows], win.at[slot, rows], wy_s.at[p, k, a], wy_r.at[p, k, a], {'tp': tp(d)}))
+                ga.append(remote(win.at[slot, rows], win.at[slot, rows], wx_s.at[p, k, a], wx_r.at[p, k, a], d2))
+                ga_in.append(remote(win.at[slot, come], win.at[slot, come], wx_s.at[p, k, a], wx_r.at[p, k, a], d2))
+            d, slot = ((-1, 0), (-1, 0), (1, 2))[a]
+            gf.append(remote(win.at[slot, rows], win.at[1, rows], wf_s.at[p, a], wf_r.at[p, a], {'tp': tp(d)}))
+            gb2.append(remote(win.at[1, rows], win.at[1, rows], wx_s.at[p, 2, a], wx_r.at[p, 2, a], d2))
+            gb_in.append(remote(win.at[1, come], win.at[1, come], wx_s.at[p, 2, a], wx_r.at[p, 2, a], d2))
+        wy.append(gy)
+        wf.append(gf)
+        wxa.append(ga)
+        wxa_in.append(ga_in)
+        wxb.append(gb2)
+        wxb_in.append(gb_in)
     for j in range(4):
-        rows, come = wslice(s + 2 * j), wslice(partner + 2 * j)
-        wd.append([remote(win.at[:, rows], win.at[:, rows], wd_s.at[j, a], wd_r.at[j, a], {'sp': partner}) for a, (w, win) in enumerate(weights)])
-        wd_in.append([remote(win.at[:, come], win.at[:, come], wd_s.at[j, a], wd_r.at[j, a], {'sp': partner}) for a, (w, win) in enumerate(weights)])
+        gd, gd_in = [], []
+        for a, (w, win, size, share) in enumerate(weights[1:]):
+            rows, come = wslice(s + 2 * j, size, share), wslice(partner + 2 * j, size, share)
+            gd.append(remote(win.at[:, rows], win.at[:, rows], wd_s.at[j, a], wd_r.at[j, a], {'sp': partner}))
+            gd_in.append(remote(win.at[:, come], win.at[:, come], wd_s.at[j, a], wd_r.at[j, a], {'sp': partner}))
+        wd.append(gd)
+        wd_in.append(gd_in)
 
     def start(copies):
         for c in copies:
@@ -95,10 +113,15 @@
 
     start(wy[0])
 
-    hot = (s * n_rows + lax.broadcasted_iota(jnp.int32, (n_sp * per, n_rows), 1) == scol_ref[...]).astype(F32).astype(BF16)
+    slots = jnp.concatenate([gpos_ref[pl.ds(c * n_tp + t, 1)] for c in range(2)], axis=1)
+    slots = jnp.transpose(jnp.broadcast_to(slots, (8, n_sp * per)))[:, :1]
+    hot = (s * n_rows + lax.broadcasted_iota(jnp.int32, (n_sp * per, n_rows), 1) == slots).astype(F32).astype(BF16)
     pick[...] = jnp.dot(hot, x_ref[...], preferred_element_type=F32).astype(BF16).reshape(n_sp, per, D)
 
-    rs = [remote(pick.at[sp(d)], rs_recv.at[s], rs_s.at[d - 1], rs_r.at[d - 1], {'sp': sp(d)}) for d in range(1, n_sp)]
+    def slot_block(dev):
+        return (dev % 2) * n_x + dev // 2
+
+    rs = [remote(pick.at[slot_block(sp(d))], rs_recv.at[s], rs_s.at[d - 1], rs_r.at[d - 1], {'sp': sp(d)}) for d in range(1, n_sp)]
     start(rs)
 
     def project(rows, pad, kdst, vdst, qdst, kdst_row, vcol, qcol):
@@ -117,7 +140,6 @@
                 for h in range(n_heads):
                     qdst[h, pl.ds(i * hd, hd), qcol] = cut[h * hd:(h + 1) * hd]
 
-    gpos = gpos_ref[...]
     mark = jnp.where(lax.broadcasted_iota(jnp.int32, (G, hd), 1) == 0, NEG, 0.0).astype(BF16)
 
     def key_pad(off):
@@ -143,7 +165,7 @@
     for c in rs:
         c.wait_recv()
     mine = core * (n_x * n_tp) + t * n_x + chip
-    rs_recv[s] = pick[s]
+    rs_recv[s] = pick[core * n_x + chip]
     xg[mine] = jnp.sum(rs_recv[...].astype(F32), axis=0).astype(BF16)
     ag = []
     for dt in range(n_tp):
@@ -154,6 +176,7 @@
     start(ag)
     arrive(wy[0])
     start(wf[0])
+    start(wxa[0])
     start(wy[1])
     arrive(halo_c)
     project(halo[0], key_pad(-WIN), k_aug, vT, None, pl.ds(0, WIN), pl.ds(0, WIN), None)
@@ -162,7 +185,7 @@
     jj = lax.broadcasted_iota(jnp.int32, (WIN, BQ), 0)
     ii = lax.broadcasted_iota(jnp.int32, (WIN, BQ), 1)
 
-    def pipeline(n_blocks, n_ch, keys, queries, values, window, finish):
+    def pipeline(n_blocks, n_ch, keys, queries, values, window, finish, hooks=None):
         def score(b, h, c, mx):
             sc = jnp.dot(keys(b, h, c), queries(b, h), preferred_element_type=F32)
             if window and c == 0:
@@ -194,6 +217,8 @@
             finish(b, h, mx, jnp.sum(ls, axis=0, keepdims=True), ac, False)
 
         def body(b, carry):
+            for at, hook in (hooks or {}).items():
+                pl.when(b == at)(hook)
             for h in range(n_heads):
                 if h + 1 < n_heads:
                     both(b, h, b, h + 1)
@@ -227,9 +252,8 @@
     agd_in = remote(xg.at[pl.ds((1 - core) * n_half, n_half)], xg.at[pl.ds((1 - core) * n_half, n_half)], agd_s.at[0], agd_r.at[0], {'sp': partner})
     agd.start()
     arrive(wf[0])
-    start(wx[0])
-    arrive(wy[1])
-    start(wf[1])
+    start(wxb[0])
+    start(wd[0])
     agd_in.wait_recv()
     gb = BQ // per
     for g in range(G // BQ):
@@ -238,6 +262,11 @@
         project(rows, jnp.zeros((BQ, hd), BF16), kg_aug, vgT, qgT, cols, cols, cols)
 
     gper = G // n_sp
+
+    def second_piece():
+        arrive(wy[1])
+        start(wf[1])
+        start(wxa[1])
 
     def gq_done(g, h, mx, ls, ac, start):
         if start:
@@ -250,14 +279,14 @@
             part[dst, pl.ds(width + 8 + h, 1)] = ls[:, cc]
 
     pipeline(G // BQ, n_rows // BQ, lambda b, h, c: k_aug[h, pl.ds(WIN + c * BQ, BQ)], lambda b, h: qgT[h, :, cols_of(b)],
-             lambda b, h, c: vT[pl.ds(h * hd, hd), pl.ds(WIN + c * BQ, BQ)], False, gq_done)
+             lambda b, h, c: vT[pl.ds(h * hd, hd), pl.ds(WIN + c * BQ, BQ)], False, gq_done, {1: second_piece})
     pt = [remote(part.at[sp(d)], part_recv.at[s], pt_s.at[d - 1], pt_r.at[d - 1], {'sp': sp(d)}) for d in range(1, n_sp)]
     for c in pt:
         c.start()
-    arrive(wf[1])
-    start(wx[1])
-    start(wd[0])
-    start(wd[1])
+    def second_forward():
+        arrive(wf[1])
+        start(wxb[1])
+        start(wd[1])
 
     def glob_done(b, h, mx, ls, ac, start):
         m_old = m_w[b, pl.ds(h, 1)]
@@ -268,7 +297,7 @@
         acc_w[b, pl.ds(h * hd, hd)] = (ac + acc_w[b, pl.ds(h * hd, hd)] * alpha) / total
 
     pipeline(n_blk, G // BQ, lambda b, h, c: kg_aug[h, pl.ds(c * BQ, BQ)], lambda b, h: qT[h, :, cols_of(b)],
-             lambda b, h, c: vgT[pl.ds(h * hd, hd), pl.ds(c * BQ, BQ)], False, glob_done)
+             lambda b, h, c: vgT[pl.ds(h * hd, hd), pl.ds(c * BQ, BQ)], False, glob_done, {2: second_forward})
 
     for c in pt:
         c.wait_recv()
@@ -283,6 +312,9 @@
     og = [remote(og_all.at[s], og_all.at[s], og_s.at[d - 1], og_r.at[d - 1], {'sp': sp(d)}) for d in range(1, n_sp)]
     for c in og:
         c.start()
+    arrive(wxa_in[0])
+    arrive(wxb_in[0])
+    start(wd[3])
     for c in og:
         c.wait_recv()
     og_ext[pl.ds(width, 16)] = jnp.ones((16, G), BF16)
@@ -304,9 +336,8 @@
         lax.fori_loop(0, n_tp, pick_block, 0)
         a2a.append([remote(o_loc.at[p, tp(-r)], o_in.at[p, r - 1], a2a_s.at[p, r - 1], a2a_r.at[p, r - 1], {'tp': tp(-r)}) for r in range(1, n_tp)])
         start(a2a[p])
-    arrive(wx_in[0])
-    start(wd[3])
-    arrive(wx_in[1])
+    arrive(wxa_in[1])
+    arrive(wxb_in[1])
     start(wd[2])
 
     def rows_of(d, p):
@@ -325,19 +356,21 @@
     for p in range(2):
         arrive(a2a[p])
         if p == 0:
+            for c in own:
+                c.wait()
             for group in wd_in:
                 arrive(group)
         mixed = jnp.zeros((BQ, D), F32)
         for r in range(n_tp):
             o_r = o_loc[p, t] if r == 0 else o_in[p, r - 1]
-            w = wo_ref[...] if r == 0 else wo_in[r - 1]
-            mixed = mixed + lax.dot_general(o_r, w, (((0,), (1,)), ((), ())), preferred_element_type=F32)
+            w = wo_own[...] if r == 0 else wo_in[r - 1]
+            mixed = mixed + lax.dot_general(o_r, w, TN, preferred_element_type=F32)
         hidden = (x_ref[rows_of(0, p)].astype(F32) + mixed).astype(BF16)
         down = jnp.zeros((BQ, D), F32)
         for r in range(n_tp):
-            z = jnp.dot(hidden, w1_ref[...] if r == 0 else w1_in[r - 1], preferred_element_type=F32)
+            z = jnp.dot(hidden, w1_own[...] if r == 0 else w1_in[r - 1], preferred_element_type=F32)
             u = jax.nn.gelu(z, approximate=True).astype(BF16)
-            down = down + jnp.dot(u, w2_ref[...] if r == 0 else w2_in[r - 1], preferred_element_type=F32)
+            down = down + jnp.dot(u, w2_own[...] if r == 0 else w2_in[r - 1], preferred_element_type=F32)
         y_ref[rows_of(0, p)] = (hidden.astype(F32) + down).astype(BF16)
         first[2 * p].start()
         first[2 * p + 1].start()
@@ -348,7 +381,7 @@
     first_in[1].wait_recv()
     first_in[2].wait_recv()
     arrive(fwd_in)
-    for c in rs + halo_c + ag + [agd] + pt + og + sum(a2a + wy + wf + wx + wd, []) + first + fwd:
+    for c in rs + halo_c + ag + [agd] + pt + og + sum(a2a + wy + wf + wxa + wxb + wd, []) + first + fwd:
         c.wait_send()
 
 
@@ -363,11 +396,8 @@
         n_x = n_sp // 2
         per = G // (n_sp * n_tp)
         dims = (n_sp, n_tp, n_heads, hd)
-        t = lax.axis_index('tp')
         ext_rows = n_rows + 2 * WIN
 
-        slots = glob_pos.reshape(2, n_tp, n_x, per)
-        slots = lax.dynamic_index_in_dim(slots, t, 1, keepdims=False).transpose(1, 0, 2).reshape(n_sp * per)
         flat = lambda w: w.reshape(D, width)
         wqv = jnp.concatenate([flat(w_query).T, flat(w_value).T], axis=0)
         vm = pl.BlockSpec(memory_space=pltpu.VMEM)
@@ -376,10 +406,11 @@
         return pl.pallas_call(
             functools.partial(layer_kernel, dims),
             out_shape=jax.ShapeDtypeStruct((n_rows, D), BF16),
-            in_specs=[vm] * 8,
+            in_specs=[vm] * 4 + [pl.BlockSpec(memory_space=pl.ANY)] * 3,
             out_specs=vm,
             scratch_shapes=[
-                pltpu.VMEM((n_tp - 1,) + w_up.shape, BF16), pltpu.VMEM((n_tp - 1,) + w_down.shape, BF16), pltpu.VMEM((n_tp - 1, D, width), BF16),
+                pltpu.VMEM(w_up.shape, BF16), pltpu.VMEM(w_down.shape, BF16), pltpu.VMEM((width, D), BF16),
+                pltpu.VMEM((n_tp - 1,) + w_up.shape, BF16), pltpu.VMEM((n_tp - 1,) + w_down.shape, BF16), pltpu.VMEM((n_tp - 1, width, D), BF16),
                 pltpu.VMEM((n_sp, per, D), BF16),
                 pltpu.VMEM((2, WIN, D), BF16), pltpu.VMEM((n_sp, per, D), BF16), pltpu.VMEM((n_sp * n_tp, per, D), BF16),
                 pltpu.VMEM((n_heads, n_rows, BQ), F32), pltpu.VMEM((n_heads, 8, BQ), F32),
@@ -392,12 +423,12 @@
                 dma((2,)), dma((2,)), dma((n_sp - 1,)), dma((n_sp - 1,)), dma((n_x * n_tp - 1,)), dma((n_x * n_tp - 1,)),
                 dma((1,)), dma((1,)), dma((n_sp - 1,)), dma((n_sp - 1,)), dma((n_sp - 1,)), dma((n_sp - 1,)),
                 dma((2, n_tp - 1)), dma((2, n_tp - 1)),
-                dma((2, 2, 3)), dma((2, 2, 3)), dma((2, 3)), dma((2, 3)), dma((2, 3)), dma((2, 3)), dma((4, 3)), dma((4, 3)),
-                dma((4,)), dma((4,)), dma((2,)), dma((2,)),
+                dma((2, 2, 3)), dma((2, 2, 3)), dma((2, 3)), dma((2, 3)), dma((2, 3, 3)), dma((2, 3, 3)), dma((4, 2)), dma((4, 2)),
+                dma((4,)), dma((4,)), dma((2,)), dma((2,)), dma((3,)),
             ],
             compiler_params=pltpu.CompilerParams(collective_id=0, has_side_effects=True, vmem_limit_bytes=62 * 1024 * 1024),
             name='layer',
-        )(tokens, wqv, flat(w_key), slots.reshape(-1, 1), glob_pos.reshape(1, G), w_up, w_down, w_out.reshape(width, D).T)
+        )(tokens, wqv, flat(w_key), glob_pos.reshape(2 * n_tp, n_x * per), w_up, w_down, w_out.reshape(width, D))
 
     row_spec = P(('dp', 'sp'), None)
     head_spec = P(None, 'tp', None)

time: 141 us -> 132 us (0.936)
  Pallas kernels: 130 us -> 124 us
  local copies, waits for them, and re-layouts: 9.14 us -> 5.63 us
    pallas_call x1, Pallas kernels: 130 us -> 124 us  [device_layer(): pl.pallas_call(functools.partial(layer_kernel, dims), out_shape=jax.Shape...]
    reshape x2 -> x0, local copies, waits for them, and re-layouts: 2.69 us -> none  [the longest x1 1.87 us: device_layer(): w_out.reshape(width, D)]
    unnamed x5 -> x1, local copies, waits for them, and re-layouts: 3.76 us -> 3.76 us
where the time goes in v3:
time: 132 us
  Pallas kernels  124 us (94%)
  local copies, waits for them, and re-layouts  5.63 us (4%)
  other arithmetic  1.9 us (1%)
    pallas_call x1, Pallas kernels, device_layer(): pl.pallas_call(functools.partial(layer_kernel, dims), out_shape=jax.Shape...  124 us
    unnamed x1, local copies, waits for them, and re-layouts  3.76 us

profile of v3, /device:TPU:97, one launch (start us, length us, event | category | flops | bytes accessed | tf_op | source)
XLA Modules:
  0.0 131.7 jit_solution(14612033389643545625)
XLA Ops:
  0.0 1.9 %copy.10.wk_ref = bf16[768,192]{1,0:T(8,128)(2,1)} copy(bf16[768,192]{0,1:T(8,128)(2,1)} %bitcast.10) | data formatting | bytes 589824 | tf_op jit(solution)/shard_map/reshape | solution.py:401
  1.9 1.9 %pad_maximum_fusion.wqv_ref = bf16[384,768]{1,0:T(8,128)(2,1)} fusion(bf16[192,768]{1,0:T(8,128)(2,1)} %bitcast.11, bf16[192,768]{1,0:T(8,128)(2,1)} %bitcast.12), kind=kLoop, calls=%fused_computation | loop fusion | flops 1179648 | bytes 1179648 | tf_op jit(solution)/shard_map/concatenate | solution.py:402
  3.8 124.1 %layer.1 = bf16[2048,768]{1,0:T(8,128)(2,1)} custom-call(bf16[2048,768]{1,0:T(8,128)(2,1)} %x_ref.1, bf16[384,768]{1,0:T(8,128)(2,1)} %pad_maximum_fusion.wqv_ref, bf16[768,192]{1,0:T(8,128)(2,1)} %copy.10.wk_ref, s32[8,128]{1,0:T(8,128)} %bitcast.13, bf16[768,768]{1,0:T(8,128)(2,1)} %w1_ref.1, bf16[768,768]{1,0:T(8,128)(2,1)} %w2_ref.1, ...), custom_call_target="tpu_custom_call" | custom-call | tf_op jit(solution)/shard_map/layer/pallas_call | solution.py:406
  127.9 3.8 %copy.12 = bf16[2048,768]{1,0:T(8,128)(2,1)} copy(bf16[2048,768]{1,0:T(8,128)(2,1)} %layer.1) | data formatting | bytes 6291456

commit v4 on v3

--- a/solution.py
+++ b/solution.py
@@ -23,7 +23,7 @@
     return pltpu.make_async_remote_copy(src_ref=src, dst_ref=dst, send_sem=send, recv_sem=recv, device_id=where, device_id_type=MESH)
 
 
-def layer_kernel(dims, x_ref, wqv_ref, wk_ref, gpos_ref, w1_ref, w2_ref, wo_ref,
+def layer_kernel(dims, x_ref, wqkv_ref, gpos_ref, w1_ref, w2_ref, wo_ref,
                  y_ref,
                  w1_own, w2_own, wo_own, w1_in, w2_in, wo_in, pick, halo, rs_recv, xg, s_scr, m_scr, qT, k_aug, vT, qgT, kg_aug, vgT, m_w, l_w, acc_w, part, part_recv,
                  og_all, og_ext, o_loc, o_in,
@@ -74,20 +74,22 @@
 
     wy, wf, wxa, wxa_in, wxb, wxb_in, wd, wd_in = [], [], [], [], [], [], [], []
     partner = 2 * chip + 1 - core
-    for p in range(2):
+    for p in range(3):
         gy, gf, ga, ga_in, gb2, gb_in = [], [], [], [], [], []
-        d2 = {'sp': sp(2 - 4 * p)}
+        d2 = {'sp': sp(2 - 2 * p)}
         for a, (w, win, size, share) in enumerate(weights):
             rows = wslice(s + 2 * p, size, share)
-            come = wslice(s - 2 if p == 0 else s + 4, size, share)
+            come = wslice(s - 2, size, share)
             for k, (d, slot) in enumerate(((-1, 0), (1, 2))):
                 gy.append(remote(w.at[rows], win.at[slot, rows], wy_s.at[p, k, a], wy_r.at[p, k, a], {'tp': tp(d)}))
-                ga.append(remote(win.at[slot, rows], win.at[slot, rows], wx_s.at[p, k, a], wx_r.at[p, k, a], d2))
-                ga_in.append(remote(win.at[slot, come], win.at[slot, come], wx_s.at[p, k, a], wx_r.at[p, k, a], d2))
             d, slot = ((-1, 0), (-1, 0), (1, 2))[a]
             gf.append(remote(win.at[slot, rows], win.at[1, rows], wf_s.at[p, a], wf_r.at[p, a], {'tp': tp(d)}))
-            gb2.append(remote(win.at[1, rows], win.at[1, rows], wx_s.at[p, 2, a], wx_r.at[p, 2, a], d2))
-            gb_in.append(remote(win.at[1, come], win.at[1, come], wx_s.at[p, 2, a], wx_r.at[p, 2, a], d2))
+            if p == (0, 0, 2)[a]:
+                for slot in (0, 2):
+                    ga.append(remote(win.at[slot, rows], win.at[slot, rows], wx_s.at[slot, a], wx_r.at[slot, a], d2))
+                    ga_in.append(remote(win.at[slot, come], win.at[slot, come], wx_s.at[slot, a], wx_r.at[slot, a], d2))
+                gb2.append(remote(win.at[1, rows], win.at[1, rows], wx_s.at[1, a], wx_r.at[1, a], d2))
+                gb_in.append(remote(win.at[1, come], win.at[1, come], wx_s.at[1, a], wx_r.at[1, a], d2))
         wy.append(gy)
         wf.append(gf)
         wxa.append(ga)
@@ -125,8 +127,8 @@
     start(rs)
 
     def project(rows, pad, kdst, vdst, qdst, kdst_row, vcol, qcol):
-        qv = lax.dot_general(wqv_ref[...], rows, NT, preferred_element_type=F32).astype(BF16)
-        kk = jnp.dot(rows, wk_ref[...], preferred_element_type=F32).astype(BF16)
+        qv = lax.dot_general(wqkv_ref[pl.ds(0, 2 * width)], rows, NT, preferred_element_type=F32).astype(BF16)
+        kk = lax.dot_general(rows, wqkv_ref[pl.ds(2 * width, width)], NT, preferred_element_type=F32).astype(BF16)
         vdst[:, vcol] = qv[width:]
         for h in range(n_heads):
             kh = kk[:, h * hd:(h + 1) * hd]
@@ -178,6 +180,7 @@
     start(wf[0])
     start(wxa[0])
     start(wy[1])
+    start(wy[2])
     arrive(halo_c)
     project(halo[0], key_pad(-WIN), k_aug, vT, None, pl.ds(0, WIN), pl.ds(0, WIN), None)
     project(halo[1], key_pad(n_rows), k_aug, vT, None, pl.ds(n_rows + WIN, WIN), pl.ds(n_rows + WIN, WIN), None)
@@ -266,7 +269,6 @@
     def second_piece():
         arrive(wy[1])
         start(wf[1])
-        start(wxa[1])
 
     def gq_done(g, h, mx, ls, ac, start):
         if start:
@@ -283,9 +285,13 @@
     pt = [remote(part.at[sp(d)], part_recv.at[s], pt_s.at[d - 1], pt_r.at[d - 1], {'sp': sp(d)}) for d in range(1, n_sp)]
     for c in pt:
         c.start()
+    def third_piece():
+        arrive(wy[2])
+        start(wf[2])
+        start(wxa[2])
+
     def second_forward():
         arrive(wf[1])
-        start(wxb[1])
         start(wd[1])
 
     def glob_done(b, h, mx, ls, ac, start):
@@ -297,8 +303,11 @@
         acc_w[b, pl.ds(h * hd, hd)] = (ac + acc_w[b, pl.ds(h * hd, hd)] * alpha) / total
 
     pipeline(n_blk, G // BQ, lambda b, h, c: kg_aug[h, pl.ds(c * BQ, BQ)], lambda b, h: qT[h, :, cols_of(b)],
-             lambda b, h, c: vgT[pl.ds(h * hd, hd), pl.ds(c * BQ, BQ)], False, glob_done, {2: second_forward})
-
+             lambda b, h, c: vgT[pl.ds(h * hd, hd), pl.ds(c * BQ, BQ)], False, glob_done, {1: third_piece, 4: second_forward})
+
+    arrive(wf[2])
+    start(wxb[2])
+    start(wd[2])
     for c in pt:
         c.wait_recv()
     part_recv[s] = part[s]
@@ -314,7 +323,6 @@
         c.start()
     arrive(wxa_in[0])
     arrive(wxb_in[0])
-    start(wd[3])
     for c in og:
         c.wait_recv()
     og_ext[pl.ds(width, 16)] = jnp.ones((16, G), BF16)
@@ -336,9 +344,9 @@
         lax.fori_loop(0, n_tp, pick_block, 0)
         a2a.append([remote(o_loc.at[p, tp(-r)], o_in.at[p, r - 1], a2a_s.at[p, r - 1], a2a_r.at[p, r - 1], {'tp': tp(-r)}) for r in range(1, n_tp)])
         start(a2a[p])
-    arrive(wxa_in[1])
-    arrive(wxb_in[1])
-    start(wd[2])
+    arrive(wxa_in[2])
+    arrive(wxb_in[2])
+    start(wd[3])
 
     def rows_of(d, p):
         return pl.ds(pl.multiple_of(tp(d) * chunk + p * BQ, BQ), BQ)
@@ -399,14 +407,14 @@
         ext_rows = n_rows + 2 * WIN
 
         flat = lambda w: w.reshape(D, width)
-        wqv = jnp.concatenate([flat(w_query).T, flat(w_value).T], axis=0)
+        wqkv = jnp.concatenate([flat(w_query).T, flat(w_value).T, flat(w_key).T], axis=0)
         vm = pl.BlockSpec(memory_space=pltpu.VMEM)
         dma = pltpu.SemaphoreType.DMA
         n_blk = n_rows // BQ
         return pl.pallas_call(
             functools.partial(layer_kernel, dims),
             out_shape=jax.ShapeDtypeStruct((n_rows, D), BF16),
-            in_specs=[vm] * 4 + [pl.BlockSpec(memory_space=pl.ANY)] * 3,
+            in_specs=[vm] * 3 + [pl.BlockSpec(memory_space=pl.ANY)] * 3,
             out_specs=vm,
             scratch_shapes=[
                 pltpu.VMEM(w_up.shape, BF16), pltpu.VMEM(w_down.shape, BF16), pltpu.VMEM((width, D), BF16),
@@ -423,12 +431,12 @@
                 dma((2,)), dma((2,)), dma((n_sp - 1,)), dma((n_sp - 1,)), dma((n_x * n_tp - 1,)), dma((n_x * n_tp - 1,)),
                 dma((1,)), dma((1,)), dma((n_sp - 1,)), dma((n_sp - 1,)), dma((n_sp - 1,)), dma((n_sp - 1,)),
                 dma((2, n_tp - 1)), dma((2, n_tp - 1)),
-                dma((2, 2, 3)), dma((2, 2, 3)), dma((2, 3)), dma((2, 3)), dma((2, 3, 3)), dma((2, 3, 3)), dma((4, 2)), dma((4, 2)),
+                dma((3, 2, 3)), dma((3, 2, 3)), dma((3, 3)), dma((3, 3)), dma((3, 3)), dma((3, 3)), dma((4, 2)), dma((4, 2)),
                 dma((4,)), dma((4,)), dma((2,)), dma((2,)), dma((3,)),
             ],
             compiler_params=pltpu.CompilerParams(collective_id=0, has_side_effects=True, vmem_limit_bytes=62 * 1024 * 1024),
             name='layer',
-        )(tokens, wqv, flat(w_key), glob_pos.reshape(2 * n_tp, n_x * per), w_up, w_down, w_out.reshape(width, D))
+        )(tokens, wqkv, glob_pos.reshape(2 * n_tp, n_x * per), w_up, w_down, w_out.reshape(width, D))
 
     row_spec = P(('dp', 'sp'), None)
     head_spec = P(None, 'tp', None)

time: 132 us -> 122 us (0.924)
  Pallas kernels: 124 us -> 116 us
  local copies, waits for them, and re-layouts: 5.63 us -> 3.76 us
    pallas_call x1, Pallas kernels: 124 us -> 116 us  [device_layer(): pl.pallas_call(functools.partial(layer_kernel, dims), out_shape=jax.Shape...]
    reshape x1 -> x0, local copies, waits for them, and re-layouts: 1.88 us -> none  [device_layer(): flat = lambda w: w.reshape(D, width)]
where the time goes in v4:
time: 122 us
  Pallas kernels  116 us (95%)
  local copies, waits for them, and re-layouts  3.76 us (3%)
  other arithmetic  2.11 us (2%)
    pallas_call x1, Pallas kernels, device_layer(): pl.pallas_call(functools.partial(layer_kernel, dims), out_shape=jax.Shape...  116 us
    unnamed x1, local copies, waits for them, and re-layouts  3.76 us

profile of v4, /device:TPU:97, one launch (start us, length us, event | category | flops | bytes accessed | tf_op | source)
XLA Modules:
  0.0 121.8 jit_solution(5350486623722424512)
XLA Ops:
  0.0 2.1 %pad_maximum_fusion.wqkv_ref = bf16[576,768]{1,0:T(8,128)(2,1)} fusion(bf16[192,768]{1,0:T(8,128)(2,1)} %bitcast.12, bf16[192,768]{1,0:T(8,128)(2,1)} %bitcast.13, bf16[192,768]{1,0:T(8,128)(2,1)} %bitcast.14), kind=kLoop, calls=%fused_computation | loop fusion | flops 2654208 | bytes 1769472 | tf_op jit(solution)/shard_map/concatenate | solution.py:410
  2.1 115.9 %layer.1 = bf16[2048,768]{1,0:T(8,128)(2,1)} custom-call(bf16[2048,768]{1,0:T(8,128)(2,1)} %x_ref.1, bf16[576,768]{1,0:T(8,128)(2,1)} %pad_maximum_fusion.wqkv_ref, s32[8,128]{1,0:T(8,128)} %bitcast.15, bf16[768,768]{1,0:T(8,128)(2,1)} %w1_ref.1, bf16[768,768]{1,0:T(8,128)(2,1)} %w2_ref.1, bf16[192,768]{1,0:T(8,128)(2,1)} %bitcast.11), custom_call_target="tpu_custom_call" | custom-call | tf_op jit(solution)/shard_map/layer/pallas_call | solution.py:414
  118.0 3.8 %copy.10 = bf16[2048,768]{1,0:T(8,128)(2,1)} copy(bf16[2048,768]{1,0:T(8,128)(2,1)} %layer.1) | data formatting | bytes 6291456

commit v5 on v4

--- a/solution.py
+++ b/solution.py
@@ -188,7 +188,7 @@
     jj = lax.broadcasted_iota(jnp.int32, (WIN, BQ), 0)
     ii = lax.broadcasted_iota(jnp.int32, (WIN, BQ), 1)
 
-    def pipeline(n_blocks, n_ch, keys, queries, values, window, finish, hooks=None):
+    def pipeline(n_blocks, n_ch, keys, queries, values, window, finish, hooks=None, after=None):
         def score(b, h, c, mx):
             sc = jnp.dot(keys(b, h, c), queries(b, h), preferred_element_type=F32)
             if window and c == 0:
@@ -227,6 +227,8 @@
                     both(b, h, b, h + 1)
                 else:
                     both(b, h, jnp.minimum(b + 1, n_blocks - 1), 0)
+            if after is not None:
+                after(b)
             return carry
 
         first(0, 0)
@@ -266,6 +268,15 @@
 
     gper = G // n_sp
 
+    def send_part(g):
+        for q in range(BQ // gper):
+            dst = g * (BQ // gper) + q
+
+            @pl.when(dst != s)
+            def _():
+                j = (dst - s + n_sp) % n_sp - 1
+                remote(part.at[dst], part_recv.at[s], pt_s.at[j], pt_r.at[j], {'sp': dst}).start()
+
     def second_piece():
         arrive(wy[1])
         start(wf[1])
@@ -281,10 +292,8 @@
             part[dst, pl.ds(width + 8 + h, 1)] = ls[:, cc]
 
     pipeline(G // BQ, n_rows // BQ, lambda b, h, c: k_aug[h, pl.ds(WIN + c * BQ, BQ)], lambda b, h: qgT[h, :, cols_of(b)],
-             lambda b, h, c: vT[pl.ds(h * hd, hd), pl.ds(WIN + c * BQ, BQ)], False, gq_done, {1: second_piece})
+             lambda b, h, c: vT[pl.ds(h * hd, hd), pl.ds(WIN + c * BQ, BQ)], False, gq_done, {1: second_piece}, send_part)
     pt = [remote(part.at[sp(d)], part_recv.at[s], pt_s.at[d - 1], pt_r.at[d - 1], {'sp': sp(d)}) for d in range(1, n_sp)]
-    for c in pt:
-        c.start()
     def third_piece():
         arrive(wy[2])
         start(wf[2])

time: 122 us -> 120 us (0.984)
  the two profiles are of different devices: /device:TPU:97 before, /device:TPU:118 now
where the time goes in v5:
time: 120 us
  Pallas kernels  114 us (95%)
  local copies, waits for them, and re-layouts  3.76 us (3%)
  other arithmetic  2.11 us (2%)
    pallas_call x1, Pallas kernels, device_layer(): pl.pallas_call(functools.partial(layer_kernel, dims), out_shape=jax.Shape...  114 us
    unnamed x1, local copies, waits for them, and re-layouts  3.76 us

profile of v5, /device:TPU:118, one launch (start us, length us, event | category | flops | bytes accessed | tf_op | source)
XLA Modules:
  0.0 120.1 jit_solution(6109606659901506212)
XLA Ops:
  0.0 2.1 %pad_maximum_fusion.wqkv_ref = bf16[576,768]{1,0:T(8,128)(2,1)} fusion(bf16[192,768]{1,0:T(8,128)(2,1)} %bitcast.12, bf16[192,768]{1,0:T(8,128)(2,1)} %bitcast.13, bf16[192,768]{1,0:T(8,128)(2,1)} %bitcast.14), kind=kLoop, calls=%fused_computation | loop fusion | flops 2654208 | bytes 1769472 | tf_op jit(solution)/shard_map/concatenate | solution.py:419
  2.1 114.2 %layer.1 = bf16[2048,768]{1,0:T(8,128)(2,1)} custom-call(bf16[2048,768]{1,0:T(8,128)(2,1)} %x_ref.1, bf16[576,768]{1,0:T(8,128)(2,1)} %pad_maximum_fusion.wqkv_ref, s32[8,128]{1,0:T(8,128)} %bitcast.15, bf16[768,768]{1,0:T(8,128)(2,1)} %w1_ref.1, bf16[768,768]{1,0:T(8,128)(2,1)} %w2_ref.1, bf16[192,768]{1,0:T(8,128)(2,1)} %bitcast.11), custom_call_target="tpu_custom_call" | custom-call | tf_op jit(solution)/shard_map/layer/pallas_call | solution.py:423
  116.3 3.8 %copy.10 = bf16[2048,768]{1,0:T(8,128)(2,1)} copy(bf16[2048,768]{1,0:T(8,128)(2,1)} %layer.1) | data formatting | bytes 6291456
